TPU v7x, 8 devices: a whole 2x2x1 slice. The times are simulated.
8 devices in a mesh: dp: 1 (over z), sw: 2 (over y), sh: 4 (over x, core).
Axes of the slice: x: 2, y: 2, z: 1, core: 2. Of those that a mesh axis runs over, the one named last changes fastest.
Arguments:
- act_in: bfloat16 [32, 48, 64, 40], P('dp', 'sh', 'sw')
- drop_mask: float32 [32, 2], P('dp')
- grad_out: bfloat16 [32, 48, 64, 40], P('dp', 'sh', 'sw')
- conv_w: bfloat16 [2, 7, 7, 40], replicated
- conv_b: float32 [2, 40], replicated
- norm_g: float32 [2, 40], replicated
- norm_b: float32 [2, 40], replicated
- fc1_w: bfloat16 [2, 40, 160], replicated
- fc1_b: float32 [2, 160], replicated
- grn_gamma: float32 [2, 160], replicated
- grn_beta: float32 [2, 160], replicated
- fc2_w: bfloat16 [2, 160, 40], replicated
- fc2_b: float32 [2, 40], replicated
Outputs:
- output 1: bfloat16 [32, 48, 64, 40], P('dp', 'sh', 'sw')
- output 2: bfloat16 [32, 48, 64, 40], P('dp', 'sh', 'sw')
- output 3: float32 [2, 7, 7, 40], P('dp')
- output 4: float32 [2, 40], P('dp')
- output 5: float32 [2, 40], P('dp')
- output 6: float32 [2, 40], P('dp')
- output 7: float32 [2, 40, 160], P('dp')
- output 8: float32 [2, 160], P('dp')
- output 9: float32 [2, 160], P('dp')
- output 10: float32 [2, 160], P('dp')
- output 11: float32 [2, 160, 40], P('dp')
- output 12: float32 [2, 40], P('dp')
All inputs are finite; a program needn't handle non-finite values.
Results may differ from a plain program's by a relative error of at most 0.0166898.
Values are sent between devices in bfloat16 or wider.
A program may use at most 1 GiB of HBM per device.

v0:
```python
import jax
import jax.numpy as jnp
from jax import lax
from jax.sharding import PartitionSpec as P

EPSILON = 1e-6
RADIUS = 3


def gelu_exact(values):
    return jax.nn.gelu(values, approximate=False)


def depthwise(padded, kernel):
    return lax.conv_general_dilated(padded, kernel[:, :, None, :], (1, 1), 'VALID',
                                    dimension_numbers=('NHWC', 'HWIO', 'NHWC'),
                                    feature_group_count=padded.shape[-1],
                                    preferred_element_type=jnp.float32)


def depthwise_wgrad(padded, cotangent):
    return lax.conv_general_dilated(padded, cotangent, (1, 1), 'VALID',
                                    dimension_numbers=('CHWN', 'IHWO', 'NHWC'),
                                    batch_group_count=padded.shape[-1],
                                    preferred_element_type=jnp.float32)[0]


def norm_stats(conv_out):
    conv32 = conv_out.astype(jnp.float32)
    centered = conv32 - jnp.mean(conv32, axis=-1, keepdims=True)
    inv_std = lax.rsqrt(jnp.mean(centered * centered, axis=-1, keepdims=True) + EPSILON)
    return centered * inv_std, inv_std


def shift_from(strip, axis_name, axis_size, downward):
    if axis_size == 1:
        return jnp.zeros_like(strip)
    if downward:
        perm_pairs = [(i, i + 1) for i in range(axis_size - 1)]
    else:
        perm_pairs = [(i + 1, i) for i in range(axis_size - 1)]
    return lax.ppermute(strip, axis_name, perm_pairs)


def with_halo(tensor, halo_width, grid_sizes):
    tile_h = tensor.shape[1]
    from_above = shift_from(tensor[:, tile_h - halo_width:], 'sh', grid_sizes[0], True)
    from_below = shift_from(tensor[:, :halo_width], 'sh', grid_sizes[0], False)
    tall_block = jnp.concatenate([from_above, tensor, from_below], axis=1)
    tile_w = tensor.shape[2]
    from_left = shift_from(tall_block[:, :, tile_w - halo_width:], 'sw', grid_sizes[1], True)
    from_right = shift_from(tall_block[:, :, :halo_width], 'sw', grid_sizes[1], False)
    return jnp.concatenate([from_left, tall_block, from_right], axis=2)


def grn_backward(d_resp32, g_act, g_norm, grn_scale, grn_gamma, cross_sum):
    mean_norm = jnp.mean(g_norm, axis=-1, keepdims=True) + EPSILON
    d_scale = grn_gamma * cross_sum
    d_gnorm = d_scale / mean_norm - jnp.sum(d_scale * g_norm, axis=-1, keepdims=True) / (mean_norm * mean_norm * g_norm.shape[-1])
    d_square = d_gnorm / (2.0 * g_norm)
    return d_resp32 * (grn_gamma * grn_scale[:, None, None, :] + 1.0) + 2.0 * g_act * d_square[:, None, None, :]


def block_forward(x_loc, mask_k, weights, grid_sizes):
    conv_w, conv_b, norm_g, norm_b, fc1_w, fc1_b, grn_gamma, grn_beta, fc2_w, fc2_b = weights
    padded = with_halo(x_loc, RADIUS, grid_sizes)
    conv_out = (depthwise(padded, conv_w) + conv_b).astype(jnp.bfloat16)
    normed = norm_stats(conv_out)[0]
    n_act = (normed * norm_g + norm_b).astype(jnp.bfloat16)
    hidden = (jnp.einsum('bhwc,ck->bhwk', n_act, fc1_w, preferred_element_type=jnp.float32) + fc1_b).astype(jnp.bfloat16)
    g_act = gelu_exact(hidden.astype(jnp.float32))
    g_norm = jnp.sqrt(lax.psum(jnp.sum(g_act * g_act, axis=(1, 2)), ('sh', 'sw')))
    grn_scale = g_norm / (jnp.mean(g_norm, axis=-1, keepdims=True) + EPSILON)
    grn_out = (grn_gamma * (g_act * grn_scale[:, None, None, :]) + grn_beta + g_act).astype(jnp.bfloat16)
    proj_out = jnp.einsum('bhwk,kc->bhwc', grn_out, fc2_w, preferred_element_type=jnp.float32) + fc2_b
    block_out = (x_loc.astype(jnp.float32) + mask_k[:, None, None, None] * proj_out).astype(jnp.bfloat16)
    return block_out, (padded, conv_out, n_act, hidden, g_norm, grn_scale, grn_out)


def block_backward(d_out, mask_k, weights, saved, grid_sizes):
    conv_w, conv_b, norm_g, norm_b, fc1_w, fc1_b, grn_gamma, grn_beta, fc2_w, fc2_b = weights
    padded, conv_out, n_act, hidden, g_norm, grn_scale, grn_out = saved
    d_resp = (mask_k[:, None, None, None] * jnp.einsum('bhwc,kc->bhwk', d_out, fc2_w, preferred_element_type=jnp.float32)).astype(jnp.bfloat16)
    per_image = jnp.einsum('bhwk,bhwc->bkc', grn_out, d_out, preferred_element_type=jnp.float32)
    grad_fc2_w = jnp.einsum('b,bkc->kc', mask_k, per_image)
    grad_fc2_b = jnp.einsum('b,bc->c', mask_k, jnp.sum(d_out, axis=(1, 2), dtype=jnp.float32))
    d_resp32 = d_resp.astype(jnp.float32)
    g_act, gelu_back = jax.vjp(gelu_exact, hidden.astype(jnp.float32))
    local_cross = jnp.sum(d_resp32 * g_act, axis=(1, 2))
    grad_grn_gamma = jnp.einsum('bk,bk->k', local_cross, grn_scale)
    grad_grn_beta = jnp.sum(d_resp32, axis=(0, 1, 2))
    cross_sum = lax.psum(local_cross, ('sh', 'sw'))
    d_gact = grn_backward(d_resp32, g_act, g_norm, grn_scale, grn_gamma, cross_sum)
    d_hidden = gelu_back(d_gact)[0].astype(jnp.bfloat16)
    grad_fc1_w = jnp.einsum('bhwc,bhwk->ck', n_act, d_hidden, preferred_element_type=jnp.float32)
    grad_fc1_b = jnp.sum(d_hidden, axis=(0, 1, 2), dtype=jnp.float32)
    d_norm32 = jnp.einsum('bhwk,ck->bhwc', d_hidden, fc1_w, preferred_element_type=jnp.float32).astype(jnp.bfloat16).astype(jnp.float32)
    normed, inv_std = norm_stats(conv_out)
    grad_norm_g = jnp.sum(d_norm32 * normed, axis=(0, 1, 2))
    grad_norm_b = jnp.sum(d_norm32, axis=(0, 1, 2))
    d_normed = d_norm32 * norm_g
    d_conv = (inv_std * (d_normed - jnp.mean(d_normed, axis=-1, keepdims=True)
                         - normed * jnp.mean(d_normed * normed, axis=-1, keepdims=True))).astype(jnp.bfloat16)
    grad_conv_b = jnp.sum(d_conv, axis=(0, 1, 2), dtype=jnp.float32)
    grad_conv_w = depthwise_wgrad(padded, d_conv)
    d_conv_pad = with_halo(d_conv, RADIUS, grid_sizes)
    d_input = (d_out.astype(jnp.float32) + depthwise(d_conv_pad, conv_w[::-1, ::-1])).astype(jnp.bfloat16)
    return d_input, (grad_conv_w, grad_conv_b, grad_norm_g, grad_norm_b, grad_fc1_w, grad_fc1_b,
                     grad_grn_gamma, grad_grn_beta, grad_fc2_w, grad_fc2_b)


def solution(mesh):
    grid_sizes = (mesh.shape['sh'], mesh.shape['sw'])
    act_spec = P('dp', 'sh', 'sw', None)
    replicated = P()

    def local_step(act_in, drop_mask, grad_out, conv_w, conv_b, norm_g, norm_b, fc1_w, fc1_b, grn_gamma, grn_beta, fc2_w, fc2_b):
        stacked = (conv_w, conv_b, norm_g, norm_b, fc1_w, fc1_b, grn_gamma, grn_beta, fc2_w, fc2_b)
        first_w = tuple(weight[0] for weight in stacked)
        second_w = tuple(weight[1] for weight in stacked)
        out_1, saved_1 = block_forward(act_in, drop_mask[:, 0], first_w, grid_sizes)
        out_2, saved_2 = block_forward(out_1, drop_mask[:, 1], second_w, grid_sizes)
        d_mid, grads_2 = block_backward(grad_out, drop_mask[:, 1], second_w, saved_2, grid_sizes)
        d_in, grads_1 = block_backward(d_mid, drop_mask[:, 0], first_w, saved_1, grid_sizes)
        summed = lax.psum(tuple(jnp.stack([first_g, second_g]) for first_g, second_g in zip(grads_1, grads_2)), ('sh', 'sw'))
        return (out_2, d_in) + summed

    return jax.shard_map(local_step, mesh=mesh,
                         in_specs=(act_spec, P('dp', None), act_spec) + (replicated,) * 10,
                         out_specs=(act_spec, act_spec) + (P('dp'),) * 10,
                         check_vma=False)
```

profile of v0, /device:TPU:0, one launch (start us, length us, event | category | flops | bytes accessed | tf_op | source)
XLA Modules:
  0.0 625.1 jit_solution(16830096404436112292)
XLA Ops:
  10.3 3.6 collective-permute-start
  27.2 4.6 collective-permute-start.2
  32.3 3.9 collective-permute-done.3
  37.9 32.1 %convert_reduce_fusion.9 = (f32[32,12,32]{0,2,1:T(8,128)S(1)}, bf16[32,12,32,40]{3,0,2,1:T(8,128)(2,1)S(1)}) fusion(f32[40]{0:T(128)S(1)} %get-tuple-element.126, bf16[7,7,1,40]{3,1,0,2:T(8,128)(2,1)S(1)} %bitcast.155, bf16[32,18,3,40]{3,0,2,1:T(8,128)(2,1)S(1)} %collective-permute-done.3, ...), kind=kOutput, calls=%fused_computation.117 | convolution fusion | flops 51873792 | bytes 2787312 | tf_op jit(solution)/shard_map/conv_general_dilated | solution.py:15
  74.5 3.9 fusion.97
  78.4 32.9 %multiply_reduce_fusion.1 = (f32[32,160]{1,0:T(8,128)S(1)}, f32[32,12,32,160]{3,2,1,0:T(8,128)}, bf16[32,12,32,160]{3,2,1,0:T(8,128)(2,1)}) fusion(f32[160]{0:T(256)S(1)} %bitcast.176, bf16[2,40,160]{2,1,0:T(8,128)(2,1)S(1)} %copy-done.47, bf16[32,12,32,40]{3,0,2,1:T(8,128)(2,1)S(1)} %fusion.97), kind=kOutput, calls=%fused_computation.96 | convolution fusion | flops 292940800 | bytes 14984192 | tf_op jit(solution)/shard_map/bhwc,ck->bhwk/dot_general | solution.py:70
  111.4 29.6 %psum.98 = f32[32,160]{1,0:T(8,128)S(1)} all-reduce(f32[32,160]{1,0:T(8,128)S(1)} %get-tuple-element.88), channel_id=1, replica_groups=mesh['dp'=1,'sw'=2,'sh'=4] {'sh','sw'}, use_global_device_ids=true, to_apply=%region_3.0 | all-reduce | flops 5120 | bytes 40960 | tf_op jit(solution)/shard_map/psum | solution.py:72
  141.9 8.7 %add_convert_fusion.2 = bf16[32,12,32,160]{3,2,1,0:T(8,128)(2,1)S(1)} fusion(f32[32,12,32,160]{3,2,1,0:T(8,128)} %get-tuple-element.89, bf16[32,12,32,160]{3,2,1,0:T(8,128)(2,1)} %get-tuple-element.135, f32[160]{0:T(256)S(1)} %bitcast.171, f32[32,160]{1,0:T(8,128)S(1)} %get-tuple-element.86, f32[160]{0:T(256)S(1)} %bitcast.157), kind=kLoop, calls=%fused_computation.95 | loop fusion | flops 15728640 | bytes 15750400 | tf_op jit(solution)/shard_map/convert_element_type | solution.py:74
  162.8 4.6 collective-permute-start.6
  173.5 8.0 %pad_maximum_fusion = bf16[32,18,38,40]{3,2,1,0:T(8,128)(2,1)S(1)} fusion(bf16[32,18,3,40]{3,2,1,0:T(4,128)(2,1)S(1)} %copy.72, bf16[32,3,32,40]{3,2,1,0:T(8,128)(2,1)S(1)} %collective-permute-done.5, bf16[32,12,32,40]{3,2,1,0:T(8,128)(2,1)S(1)} %add_convert_fusion.6, bf16[32,3,32,40]{3,2,1,0:T(8,128)(2,1)S(1)} %collective-permute-done.4, ...), kind=kLoop, calls=%fused_computation.150 | loop fusion | flops 8755200 | bytes 3502080 | tf_op jit(solution)/shard_map/concatenate | solution.py:53
  181.5 31.3 %convert_reduce_fusion.8 = (f32[32,12,32]{0,2,1:T(8,128)S(1)}, bf16[32,12,32,40]{3,0,2,1:T(8,128)(2,1)S(1)}) fusion(f32[40]{0:T(128)S(1)} %copy-done.81, bf16[7,7,1,40]{3,1,0,2:T(8,128)(2,1)S(1)} %bitcast.153, bf16[32,18,38,40]{3,2,1,0:T(8,128)(2,1)S(1)} %pad_maximum_fusion), kind=kOutput, calls=%fused_computation.115 | convolution fusion | flops 50122752 | bytes 2787312 | tf_op jit(solution)/shard_map/conv_general_dilated | solution.py:15
  216.6 4.3 fusion.91
  223.2 33.6 %fusion.73 = (f32[32,160]{1,0:T(8,128)}, f32[32,160]{1,0:T(8,128)}, f32[160]{0:T(256)}, f32[32,12,32,160]{3,2,1,0:T(8,128)}, bf16[32,12,32,160]{3,2,1,0:T(8,128)(2,1)}) fusion(bf16[32,12,32,160]{3,2,1,0:T(8,128)(2,1)S(1)} %add_convert_fusion.1, bf16[32,12,32,40]{3,2,1,0:T(8,128)(2,1)S(1)} %copy-done.11, bf16[2,160,40]{1,2,0:T(8,128)(2,1)S(1)} %copy-done.34, ...), kind=kOutput, calls=%fused_computation.85 | convolution fusion | flops 300799840 | bytes 21296256 | tf_op jit(solution)/shard_map/bhwc,kc->bhwk/dot_general | solution.py:83
  256.8 34.7 %all-reduce.1 = (f32[32,160]{1,0:T(8,128)}, f32[32,160]{1,0:T(8,128)}) all-reduce(f32[32,160]{1,0:T(8,128)} %get-tuple-element.49, f32[32,160]{1,0:T(8,128)} %get-tuple-element.48), channel_id=1, replica_groups=mesh['dp'=1,'sw'=2,'sh'=4] {'sh','sw'}, use_global_device_ids=true, to_apply=%region_8.0 | all-reduce | flops 10240 | bytes 81920 | tf_op jit(solution)/shard_map/psum | solution.py:72
  294.7 14.4 %convert_reduce_fusion.2 = (f32[160]{0:T(256)}, bf16[32,12,32,160]{3,2,1,0:T(8,128)(2,1)S(1)}, bf16[32,12,32,160]{3,2,1,0:T(8,128)(2,1)S(1)}) fusion(f32[32,12,32,160]{3,2,1,0:T(8,128)} %get-tuple-element.87, f32[32,160]{1,0:T(8,128)S(1)} %get-tuple-element.120, f32[32,160]{1,0:T(8,128)S(1)} %get-tuple-element.119, ...), kind=kLoop, calls=%fused_computation.88 | loop fusion | flops 53084000 | bytes 23656320 | tf_op jit(solution)/shard_map/reduce_sum | solution.py:96
  309.2 9.4 %fusion.106 = (f32[40]{0:T(128)}, f32[32,12,32]{0,2,1:T(8,128)S(1)}, f32[32,12,32]{0,2,1:T(8,128)S(1)}, f32[40]{0:T(128)}, bf16[32,12,32,40]{3,0,2,1:T(8,128)(2,1)S(1)}) fusion(bf16[32,12,32,40]{3,0,2,1:T(8,128)(2,1)S(1)} %get-tuple-element.137, f32[32,12,32]{0,2,1:T(8,128)S(1)} %add_rsqrt_fusion, f32[32,12,32]{0,2,1:T(8,128)S(1)} %broadcast_multiply_fusion.4, ...), kind=kOutput, calls=%fused_computation.142 | convolution fusion | flops 163160000 | bytes 10933056 | tf_op jit(solution)/shard_map/bhwk,ck->bhwc/dot_general | solution.py:97
  318.6 8.5 %convert_reduce_fusion.10 = (f32[40]{0:T(128)}, bf16[32,12,32,40]{3,0,2,1:T(8,128)(2,1)S(1)}) fusion(f32[32,12,32]{0,2,1:T(8,128)S(1)} %broadcast_multiply_fusion.2, f32[32,12,32]{0,2,1:T(8,128)S(1)} %broadcast_multiply_fusion.4, bf16[32,12,32,40]{3,0,2,1:T(8,128)(2,1)S(1)} %get-tuple-element.137, f32[32,12,32]{0,2,1:T(8,128)S(1)} %broadcast_multiply_fusion.3, ...), kind=kLoop, calls=%fused_computation.144 | loop fusion | flops 5898200 | bytes 3146048 | tf_op jit(solution)/shard_map/reduce_sum | solution.py:104
  327.4 34.1 %fusion.136 = f32[1,7,7,40]{3,0,2,1:T(1,128)} fusion(bf16[32,12,32,40]{3,0,2,1:T(8,128)(2,1)S(1)} %get-tuple-element.84, bf16[32,18,38,40]{3,2,1,0:T(8,128)(2,1)} %copy-done.17), kind=kOutput, calls=%fused_computation.180 | convolution fusion | flops 48168960 | bytes 2741920 | tf_op jit(solution)/shard_map/conv_general_dilated | solution.py:22
  361.5 4.4 fusion.168
  377.5 6.1 collective-permute-start.10
  385.9 4.0 copy.113
  389.9 25.7 %convert_reduce_fusion.6 = (bf16[32,40]{1,0:T(8,128)(2,1)S(1)}, bf16[32,12,32,40]{3,0,2,1:T(8,128)(2,1)S(1)}) fusion(bf16[7,7,1,40]{3,1,0,2:T(8,128)(2,1)S(1)} %bitcast.164, bf16[32,18,3,40]{3,0,2,1:T(8,128)(2,1)} %collective-permute-done.11, bf16[32,3,32,40]{3,0,2,1:T(8,128)(2,1)S(1)} %collective-permute-done.9, bf16[32,12,32,40]{3,0,2,1:T(8,128)(2,1)} %copy-done.10, ...), kind=kOutput, calls=%fused_computation.110 | convolution fusion | flops 54127360 | bytes 3723600 | tf_op jit(solution)/shard_map/conv_general_dilated | solution.py:15
  415.7 11.9 %convert_reduce_fusion = (f32[160]{0:T(256)S(1)}, f32[32,160]{1,0:T(8,128)S(1)}, bf16[32,12,32,160]{3,2,1,0:T(8,128)(2,1)}) fusion(f32[32,12,32,160]{3,2,1,0:T(8,128)} %get-tuple-element.89, bf16[32,12,32,160]{3,2,1,0:T(8,128)(2,1)S(1)} %bitcast.149, bf16[2,160,40]{1,2,0:T(8,128)(2,1)S(1)} %copy-done.35, bf16[32,12,32,40]{3,0,2,1:T(8,128)(2,1)S(1)} %get-tuple-element.143, ...), kind=kOutput, calls=%fused_computation | convolution fusion | flops 174975840 | bytes 21275776 | tf_op jit(solution)/shard_map/bhwc,kc->bhwk/dot_general | solution.py:83
  427.5 30.2 %psum.101 = f32[32,160]{1,0:T(8,128)S(1)} all-reduce(f32[32,160]{1,0:T(8,128)S(1)} %get-tuple-element.55), channel_id=1, replica_groups=mesh['dp'=1,'sw'=2,'sh'=4] {'sh','sw'}, use_global_device_ids=true, to_apply=%region_16.0 | all-reduce | flops 5120 | bytes 40960 | tf_op jit(solution)/shard_map/psum | solution.py:92
  458.1 13.3 %convert_reduce_fusion.3 = (f32[160]{0:T(256)S(1)}, bf16[32,12,32,160]{3,2,1,0:T(8,128)(2,1)S(1)}) fusion(f32[32,12,32,160]{3,2,1,0:T(8,128)} %get-tuple-element.89, f32[32,160]{1,0:T(8,128)S(1)} %divide_multiply_fusion, f32[32,160]{1,0:T(8,128)S(1)} %copy-done.32, bf16[32,12,32,160]{3,2,1,0:T(8,128)(2,1)} %get-tuple-element.140, ...), kind=kLoop, calls=%fused_computation.89 | loop fusion | flops 43253600 | bytes 19702400 | tf_op jit(solution)/shard_map/reduce_sum | solution.py:96
  471.5 9.5 %fusion.107 = (f32[40]{0:T(128)S(1)}, f32[32,12,32]{0,2,1:T(8,128)S(1)}, f32[32,12,32]{0,2,1:T(8,128)S(1)}, f32[40]{0:T(128)S(1)}, bf16[32,12,32,40]{3,0,2,1:T(8,128)(2,1)}) fusion(bf16[32,12,32,40]{3,0,2,1:T(8,128)(2,1)S(1)} %copy-done.4, f32[32,12,32]{0,2,1:T(8,128)S(1)} %copy-done.21, f32[32,12,32]{0,2,1:T(8,128)S(1)} %copy-done.19, ...), kind=kOutput, calls=%fused_computation.143 | convolution fusion | flops 163160000 | bytes 10933056 | tf_op jit(solution)/shard_map/bhwk,ck->bhwc/dot_general | solution.py:97
  481.1 3.7 fusion.165
  487.1 9.3 %convert_reduce_fusion.11 = (f32[40]{0:T(128)S(1)}, bf16[32,12,32,40]{3,0,2,1:T(8,128)(2,1)S(1)}) fusion(f32[32,12,32]{0,2,1:T(8,128)S(1)} %broadcast_multiply_fusion, f32[32,12,32]{0,2,1:T(8,128)S(1)} %copy-done.19, bf16[32,12,32,40]{3,0,2,1:T(8,128)(2,1)S(1)} %copy-done.4, f32[32,12,32]{0,2,1:T(8,128)S(1)} %broadcast_multiply_fusion.1, ...), kind=kLoop, calls=%fused_computation.145 | loop fusion | flops 5898200 | bytes 3146048 | tf_op jit(solution)/shard_map/reduce_sum | solution.py:104
  503.8 35.6 %fusion.145 = f32[1,7,7,40]{3,0,2,1:T(1,128)S(1)} fusion(bf16[32,12,32,40]{3,0,2,1:T(8,128)(2,1)S(1)} %get-tuple-element.82, bf16[32,18,3,40]{3,0,2,1:T(8,128)(2,1)S(1)} %copy-done.83, bf16[32,18,32,40]{3,0,2,1:T(8,128)(2,1)S(1)} %bitcast.151, bf16[32,18,3,40]{3,0,2,1:T(8,128)(2,1)S(1)} %copy-done.85), kind=kOutput, calls=%fused_computation.189 | convolution fusion | flops 49920000 | bytes 2741920 | tf_op jit(solution)/shard_map/conv_general_dilated | solution.py:22
  547.7 6.1 collective-permute-start.14
  563.2 24.1 %fusion.103 = bf16[32,12,32,40]{3,0,2,1:T(8,128)(2,1)S(1)} fusion(bf16[32,12,32,40]{3,0,2,1:T(8,128)(2,1)} %copy-done.15, bf16[32,18,3,40]{3,0,2,1:T(8,128)(2,1)} %collective-permute-done.15, bf16[32,3,32,40]{3,0,2,1:T(8,128)(2,1)} %copy-done.24, bf16[32,12,32,40]{3,0,2,1:T(8,128)(2,1)S(1)} %get-tuple-element.82, bf16[32,3,32,40]{3,0,2,1:T(8,128)(2,1)} %copy-done.25, ...), kind=kOutput, calls=%fused_computation.139 | convolution fusion | flops 53145600 | bytes 3721040 | tf_op jit(solution)/shard_map/conv_general_dilated | solution.py:15
  590.3 14.7 %all-reduce.4.cloned.1.call-done = (f32[2,7,7,40]{3,0,2,1:T(2,128)}, f32[2,40]{1,0:T(2,128)}, f32[2,40]{1,0:T(2,128)}, f32[2,40]{1,0:T(2,128)}, f32[2,40,160]{2,...) async-done(((f32[2,7,7,40]{3,0,2,1:T(2,128)}, f32[2,40]{1,0:T(2,128)}, ...) | async-done | bytes 123216 | tf_op jit(solution)/shard_map/psum | solution.py:125
  (297 shorter events, 108.6 us)
Async XLA Ops:
  7.3 597.7 %all-reduce.4.cloned.1.call-start = ((), (), s32[]{:S(2)}) async-start(), calls=%async_computation | async-start | bytes 448512 | tf_op jit(solution)/shard_map/psum | solution.py:125
  10.3 10.8 %collective-permute-start = (bf16[32,3,32,40]{3,0,2,1:T(8,128)(2,1)}, bf16[32,3,32,40]{3,0,2,1:T(8,128)(2,1)}, u32[]{:S(2)}, u32[]{:S(2)}) collective-permute-start(bf16[32,3,32,40]{3,0,2,1:T(8,128)(2,1)} %copy.167), channel_id=1, source_target_pairs={{0,1},{1,2},{2,3},{4,5},{5,6},{6,7}} | collective-permute-start | bytes 737288 | tf_op jit(solution)/shard_map/ppermute | solution.py:42
  15.1 9.4 %collective-permute-start.1 = (bf16[32,3,32,40]{3,0,2,1:T(8,128)(2,1)}, bf16[32,3,32,40]{3,0,2,1:T(8,128)(2,1)}, u32[]{:S(2)}, u32[]{:S(2)}) collective-permute-start(bf16[32,3,32,40]{3,0,2,1:T(8,128)(2,1)} %copy.168), channel_id=1, source_target_pairs={{1,0},{2,1},{3,2},{5,4},{6,5},{7,6}} | collective-permute-start | bytes 737288 | tf_op jit(solution)/shard_map/ppermute | solution.py:42
  19.3 50.8 %copy-start.36 = (bf16[1,7,7,40]{3,2,1,0:T(8,128)(2,1)}, bf16[1,7,7,40]{3,2,1,0:T(8,128)(2,1)S(1)}, u32[]{:S(2)}) copy-start(bf16[1,7,7,40]{3,2,1,0:T(8,128)(2,1)S(1)} %copy.188) | copy-start | bytes 11764
  21.1 52.7 %copy-start.51 = (f32[40]{0:T(128)}, f32[40]{0:T(128)S(1)}, u32[]{:S(2)}) copy-start(f32[40]{0:T(128)S(1)} %get-tuple-element.144) | copy-start | bytes 484
  25.8 44.2 %copy-start.27 = (bf16[32,18,32,40]{3,0,2,1:T(8,128)(2,1)}, bf16[32,18,32,40]{3,0,2,1:T(8,128)(2,1)S(1)}, u32[]{:S(2)}) copy-start(bf16[32,18,32,40]{3,0,2,1:T(8,128)(2,1)S(1)} %constant_dynamic-update-slice_fusion) | copy-start | bytes 4423684
  25.9 10.3 %collective-permute-start.3 = (bf16[32,18,3,40]{3,0,2,1:T(8,128)(2,1)S(1)}, bf16[32,18,3,40]{3,0,2,1:T(8,128)(2,1)S(1)}, u32[]{:S(2)}, u32[]{:S(2)}) collective-permute-start(bf16[32,18,3,40]{3,0,2,1:T(8,128)(2,1)S(1)} %get-tuple-element.98), channel_id=1, source_target_pairs={{4,0},{5,1},{6,2},{7,3}} | collective-permute-start | bytes 414728 | tf_op jit(solution)/shard_map/ppermute | solution.py:42
  27.2 10.7 %collective-permute-start.2 = (bf16[32,18,3,40]{3,0,2,1:T(8,128)(2,1)S(1)}, bf16[32,18,3,40]{3,0,2,1:T(8,128)(2,1)S(1)}, u32[]{:S(2)}, u32[]{:S(2)}) collective-permute-start(bf16[32,18,3,40]{3,0,2,1:T(8,128)(2,1)S(1)} %get-tuple-element.97), channel_id=1, source_target_pairs={{0,4},{1,5},{2,6},{3,7}} | collective-permute-start | bytes 414728 | tf_op jit(solution)/shard_map/ppermute | solution.py:42
  70.1 41.3 %copy-start.3 = (bf16[32,12,32,40]{3,0,2,1:T(8,128)(2,1)}, bf16[32,12,32,40]{3,0,2,1:T(8,128)(2,1)S(1)}, u32[]{:S(2)}) copy-start(bf16[32,12,32,40]{3,0,2,1:T(8,128)(2,1)S(1)} %get-tuple-element.134) | copy-start | bytes 2949124
  78.4 62.7 %copy-start.38 = (f32[1,160]{1,0:T(1,128)S(1)}, f32[1,160]{1,0:T(1,128)}, u32[]{:S(2)}) copy-start(f32[1,160]{1,0:T(1,128)} %get-tuple-element.114) | copy-start | bytes 1924
  78.4 63.4 %copy-start.60 = (f32[1,160]{1,0:T(1,128)S(1)}, f32[1,160]{1,0:T(1,128)}, u32[]{:S(2)}) copy-start(f32[1,160]{1,0:T(1,128)} %get-tuple-element.116) | copy-start | bytes 1924
  154.2 6.5 %collective-permute-start.5 = (bf16[32,3,32,40]{3,2,1,0:T(8,128)(2,1)S(1)}, bf16[32,3,32,40]{3,2,1,0:T(8,128)(2,1)S(1)}, u32[]{:S(2)}, u32[]{:S(2)}) collective-permute-start(bf16[32,3,32,40]{3,2,1,0:T(8,128)(2,1)S(1)} %get-tuple-element.104), channel_id=1, source_target_pairs={{1,0},{2,1},{3,2},{5,4},{6,5},{7,6}} | collective-permute-start | bytes 737288 | tf_op jit(solution)/shard_map/ppermute | solution.py:42
  155.6 5.1 collective-permute-start.4
  161.4 10.2 %collective-permute-start.7 = (bf16[32,18,3,40]{3,0,2,1:T(8,128)(2,1)S(1)}, bf16[32,18,3,40]{3,0,2,1:T(8,128)(2,1)S(1)}, u32[]{:S(2)}, u32[]{:S(2)}) collective-permute-start(bf16[32,18,3,40]{3,0,2,1:T(8,128)(2,1)S(1)} %copy.70), channel_id=1, source_target_pairs={{4,0},{5,1},{6,2},{7,3}} | collective-permute-start | bytes 414728 | tf_op jit(solution)/shard_map/ppermute | solution.py:42
  162.8 10.4 %collective-permute-start.6 = (bf16[32,18,3,40]{3,0,2,1:T(8,128)(2,1)S(1)}, bf16[32,18,3,40]{3,0,2,1:T(8,128)(2,1)S(1)}, u32[]{:S(2)}, u32[]{:S(2)}) collective-permute-start(bf16[32,18,3,40]{3,0,2,1:T(8,128)(2,1)S(1)} %copy.69), channel_id=1, source_target_pairs={{0,4},{1,5},{2,6},{3,7}} | collective-permute-start | bytes 414728 | tf_op jit(solution)/shard_map/ppermute | solution.py:42
  223.2 68.4 %copy-start.44 = (f32[1,160]{1,0:T(1,128)S(1)}, f32[1,160]{1,0:T(1,128)}, u32[]{:S(2)}) copy-start(f32[1,160]{1,0:T(1,128)} %get-tuple-element.113) | copy-start | bytes 1924
  223.2 71.6 %copy-start.56 = (f32[1,160]{1,0:T(1,128)S(1)}, f32[1,160]{1,0:T(1,128)}, u32[]{:S(2)}) copy-start(f32[1,160]{1,0:T(1,128)} %get-tuple-element.115) | copy-start | bytes 1924
  327.1 48.1 %copy-start.10 = (bf16[32,12,32,40]{3,0,2,1:T(8,128)(2,1)}, bf16[32,12,32,40]{3,0,2,1:T(8,128)(2,1)S(1)}, u32[]{:S(2)}) copy-start(bf16[32,12,32,40]{3,0,2,1:T(8,128)(2,1)S(1)} %get-tuple-element.84) | copy-start | bytes 2949124
  365.9 9.2 %collective-permute-start.9 = (bf16[32,3,32,40]{3,0,2,1:T(8,128)(2,1)S(1)}, bf16[32,3,32,40]{3,0,2,1:T(8,128)(2,1)S(1)}, u32[]{:S(2)}, u32[]{:S(2)}) collective-permute-start(bf16[32,3,32,40]{3,0,2,1:T(8,128)(2,1)S(1)} %get-tuple-element.102), channel_id=1, source_target_pairs={{1,0},{2,1},{3,2},{5,4},{6,5},{7,6}} | collective-permute-start | bytes 737288 | tf_op jit(solution)/shard_map/ppermute | solution.py:42
  367.2 7.9 %collective-permute-start.8 = (bf16[32,3,32,40]{3,0,2,1:T(8,128)(2,1)S(1)}, bf16[32,3,32,40]{3,0,2,1:T(8,128)(2,1)S(1)}, u32[]{:S(2)}, u32[]{:S(2)}) collective-permute-start(bf16[32,3,32,40]{3,0,2,1:T(8,128)(2,1)S(1)} %get-tuple-element.101), channel_id=1, source_target_pairs={{0,1},{1,2},{2,3},{4,5},{5,6},{6,7}} | collective-permute-start | bytes 737288 | tf_op jit(solution)/shard_map/ppermute | solution.py:42
  376.2 13.7 %collective-permute-start.11 = (bf16[32,18,3,40]{3,0,2,1:T(8,128)(2,1)}, bf16[32,18,3,40]{3,0,2,1:T(8,128)(2,1)}, u32[]{:S(2)}, u32[]{:S(2)}) collective-permute-start(bf16[32,18,3,40]{3,0,2,1:T(8,128)(2,1)} %get-tuple-element.94), channel_id=1, source_target_pairs={{4,0},{5,1},{6,2},{7,3}} | collective-permute-start | bytes 414728 | tf_op jit(solution)/shard_map/ppermute | solution.py:42
  377.5 12.4 %collective-permute-start.10 = (bf16[32,18,3,40]{3,0,2,1:T(8,128)(2,1)S(1)}, bf16[32,18,3,40]{3,0,2,1:T(8,128)(2,1)}, u32[]{:S(2)}, u32[]{:S(2)}) collective-permute-start(bf16[32,18,3,40]{3,0,2,1:T(8,128)(2,1)S(1)} %get-tuple-element.93), channel_id=1, source_target_pairs={{0,4},{1,5},{2,6},{3,7}} | collective-permute-start | bytes 414728 | tf_op jit(solution)/shard_map/ppermute | solution.py:42
  415.6 42.1 %copy-start.23 = (f32[32,160]{1,0:T(8,128)S(1)}, f32[32,160]{1,0:T(8,128)}, u32[]{:S(2)}) copy-start(f32[32,160]{1,0:T(8,128)} %copy-done.22) | copy-start | bytes 61444
  415.6 42.1 %copy-start.39 = (f32[1,160]{1,0:T(1,128)S(1)}, f32[1,160]{1,0:T(1,128)}, u32[]{:S(2)}) copy-start(f32[1,160]{1,0:T(1,128)} %get-tuple-element.114) | copy-start | bytes 1924
  415.6 42.3 %copy-start.78 = (f32[32]{0:T(128)S(1)}, f32[32]{0:T(128)}, u32[]{:S(2)}) copy-start(f32[32]{0:T(128)} %copy-done.77) | copy-start | bytes 388
  415.6 42.3 %copy-start.62 = (f32[32]{0:T(128)S(1)}, f32[32]{0:T(128)}, u32[]{:S(2)}) copy-start(f32[32]{0:T(128)} %copy-done.61) | copy-start | bytes 388
  415.6 42.4 %copy-start.32 = (f32[32,160]{1,0:T(8,128)S(1)}, f32[32,160]{1,0:T(8,128)}, u32[]{:S(2)}) copy-start(f32[32,160]{1,0:T(8,128)} %get-tuple-element.85) | copy-start | bytes 61444
  496.8 47.6 %collective-permute-start.13 = (bf16[32,3,32,40]{3,0,2,1:T(8,128)(2,1)S(1)}, bf16[32,3,32,40]{3,0,2,1:T(8,128)(2,1)S(1)}, u32[]{:S(2)}, u32[]{:S(2)}) collective-permute-start(bf16[32,3,32,40]{3,0,2,1:T(8,128)(2,1)S(1)} %get-tuple-element.100), channel_id=1, source_target_pairs={{1,0},{2,1},{3,2},{5,4},{6,5},{7,6}} | collective-permute-start | bytes 737288 | tf_op jit(solution)/shard_map/ppermute | solution.py:42
  498.1 46.3 %collective-permute-start.12 = (bf16[32,3,32,40]{3,0,2,1:T(8,128)(2,1)S(1)}, bf16[32,3,32,40]{3,0,2,1:T(8,128)(2,1)S(1)}, u32[]{:S(2)}, u32[]{:S(2)}) collective-permute-start(bf16[32,3,32,40]{3,0,2,1:T(8,128)(2,1)S(1)} %get-tuple-element.99), channel_id=1, source_target_pairs={{0,1},{1,2},{2,3},{4,5},{5,6},{6,7}} | collective-permute-start | bytes 737288 | tf_op jit(solution)/shard_map/ppermute | solution.py:42
  503.8 50.0 %copy-start.70 = (f32[1,40]{1,0:T(1,128)S(1)}, f32[1,40]{1,0:T(1,128)}, u32[]{:S(2)}) copy-start(f32[1,40]{1,0:T(1,128)} %fusion.194) | copy-start | bytes 484
  546.4 14.1 %collective-permute-start.15 = (bf16[32,18,3,40]{3,0,2,1:T(8,128)(2,1)}, bf16[32,18,3,40]{3,0,2,1:T(8,128)(2,1)}, u32[]{:S(2)}, u32[]{:S(2)}) collective-permute-start(bf16[32,18,3,40]{3,0,2,1:T(8,128)(2,1)} %get-tuple-element.92), channel_id=1, source_target_pairs={{4,0},{5,1},{6,2},{7,3}} | collective-permute-start | bytes 414728 | tf_op jit(solution)/shard_map/ppermute | solution.py:42
  547.7 15.5 %collective-permute-start.14 = (bf16[32,18,3,40]{3,0,2,1:T(8,128)(2,1)}, bf16[32,18,3,40]{3,0,2,1:T(8,128)(2,1)}, u32[]{:S(2)}, u32[]{:S(2)}) collective-permute-start(bf16[32,18,3,40]{3,0,2,1:T(8,128)(2,1)} %get-tuple-element.91), channel_id=1, source_target_pairs={{0,4},{1,5},{2,6},{3,7}} | collective-permute-start | bytes 414728 | tf_op jit(solution)/shard_map/ppermute | solution.py:42
  (77 other events, 1307.7 us)
Sparse Core Ops, SparseCore 0:
  558.5 46.3 all-reduce.3
where the time goes:
time: 630 us; the launch traced here: 625 us
  matrix products  304 us (48%)
  blocking collectives  94.5 us (15%)
  other arithmetic  93 us (15%)
  starting transfers between devices  45 us (7%)
  local copies, waits for them, and re-layouts  42.4 us (7%)
  waiting for transfers between devices  29.9 us (5%)
  between operations  15.8 us (3%)
    conv_general_dilated x4, matrix products, depthwise(): lax.conv_general_dilated(padded, kernel[:, :, None, :], (1, 1), 'VALID',...  113 us
    conv_general_dilated x2, matrix products, depthwise_wgrad(): lax.conv_general_dilated(padded, cotangent, (1, 1), 'VALID', dimension_nu...  69.7 us
    psum x2, blocking collectives, block_forward(): lax.psum(jnp.sum(g_act * g_act, axis=(1, 2)), ('sh', 'sw'))  64.3 us
    dot_general x2, matrix products, block_backward(): jnp.einsum('bhwc,kc->bhwk', d_out, fc2_w, preferred_element_type=jnp.floa...  45.5 us
    ppermute x16, starting transfers between devices, shift_from(): return lax.ppermute(strip, axis_name, perm_pairs)  45 us
    dot_general x2, matrix products, block_forward(): jnp.einsum('bhwc,ck->bhwk', n_act, fc1_w, preferred_element_type=jnp.floa...  35.1 us
    psum x1, blocking collectives, block_backward(): cross_sum = lax.psum(local_cross, ('sh', 'sw'))  30.2 us
    reduce_sum x2, other arithmetic, block_backward(): grad_fc1_b = jnp.sum(d_hidden, axis=(0, 1, 2), dtype=jnp.float32)  27.8 us
  transfers between devices with their start and end apart: 17, of which 7 were waited for; matrix products, arithmetic and copies ran while one was open for 16% of the time, Pallas kernels for 0%

commit v1 on v0

v1 whole, which is shorter than its diff:
```python
import functools

import jax
import jax.numpy as jnp
import numpy as np
from jax import lax
from jax.experimental import pallas as pl
from jax.experimental.pallas import tpu as pltpu
from jax.sharding import PartitionSpec as P

EPS = 1e-6
F32 = jnp.float32
BF16 = jnp.bfloat16
MESH = pl.DeviceIdType.MESH
NG = 5
NPAIR = 24
ROWS = 224
KEEP = 4.0 / 3.0
FC1B, GAMMA, BETA, CONVB, NORMG, NORMB, FC2B = 0, 160, 320, 480, 520, 560, 600


LANE = 128
PXL = 256
PXP = 512
SUB = 8
CH = 40
HID = 160
IMG = 32
PR = 16
TQ = 96
CHP = 48
BAND = 1024
PIX = 384
HIDP = 176
CHQ = 88
HALFL = 64
PADH = 12
ZERO = 0.0
ONE = 1.0
TAP = 7
TILEH = 6
QUAD = 4
RAD = 3
PAIR = 2
I0 = 0
I1 = 1


def nt_dot(a, b):
    return lax.dot_general(a, b, (((I1,), (I1,)), ((), ())), preferred_element_type=F32)


def dot(a, b):
    return jnp.dot(a, b, preferred_element_type=F32)


def kernel(xin, gin, mask_in, taps, b_fc1, gamma, beta, b_conv, g_norm, b_norm, b_fc2, w1, w2t,
           y_out, dx_out, gr_out,
           xf, gout, mask, eb, cols, w1t, w2, x1, x2, dp, dbuf, nbuf, hbuf, drbuf, dmid, tbuf,
           acc_g2, acc_cross, acc_beta, acc_n, acc_f1, acc_f2, gvec, sbuf, gnbuf, qbuf,
           ru, rd, rc, sc, sa, ra, gb, grx, gs,
           hs_sem, hr_sem, as_sem, ar_sem, gs_sem, gr_sem, as2_sem, ar2_sem):
    sw = lax.axis_index('sw')
    sh = lax.axis_index('sh')
    me = sw * QUAD + sh
    other_w = I1 - sw

    def peer(d):
        f = lax.rem(me + d, SUB)
        return {'sw': f // QUAD, 'sh': lax.rem(f, QUAD)}

    barrier = pltpu.get_barrier_semaphore()
    for d in range(I1, SUB):
        pl.semaphore_signal(barrier, inc=I1, device_id=peer(d), device_id_type=MESH)
    pl.semaphore_wait(barrier, TAP)

    def setup():
        spots = ((b_fc1, FC1B), (gamma, GAMMA), (beta, BETA), (b_conv, CONVB),
                 (g_norm, NORMG), (b_norm, NORMB), (b_fc2, FC2B))
        for k in range(PAIR):
            for ref, at in spots:
                n = ref.shape[I1]
                row = jnp.broadcast_to(ref[k:k + I1, :], (LANE, n))
                cols[k, at:at + n, :] = jnp.transpose(row)
            m = jnp.concatenate([mask_in[k:k + I1, :]] * SUB, axis=I1)
            mask[k] = jnp.broadcast_to(m, (SUB, PXL))
            w1t[k] = jnp.transpose(jnp.concatenate([w1[k].astype(F32), jnp.zeros((SUB, HID), F32)], axis=I0)).astype(BF16)
            w2[k] = jnp.transpose(w2t[k].astype(F32)).astype(BF16)
        eb[...] = jnp.zeros_like(eb)
        place = lax.broadcasted_iota(jnp.int32, (PAIR, LANE), I1) // SUB

        def taps_row(i, carry):
            rows = [jnp.concatenate([taps[i, j].astype(F32), jnp.zeros((PAIR, CHQ), F32)], axis=I1) for j in range(TAP)]
            for g in range(NG):
                fwd = jnp.zeros((PAIR, LANE), F32)
                bwd = jnp.zeros((PAIR, LANE), F32)
                for j in range(TAP):
                    fwd = jnp.where(place == j, pltpu.roll(rows[j], (LANE + SUB * (j - g)) % LANE, I1), fwd)
                    bwd = jnp.where(place == TILEH - j, pltpu.roll(rows[j], (LANE + SUB * (TILEH - j - g)) % LANE, I1), bwd)
                eb[I0, g, i, I0:PAIR, :] = fwd
                eb[I1, g, TILEH - i, I0:PAIR, :] = bwd
            return carry
        lax.fori_loop(I0, TAP, taps_row, I0)

    def load_tiles(src, store):
        def widen(b, carry):
            xf[pl.ds(pl.multiple_of(b * PIX, PIX), PIX), :] = src[b].reshape(PIX, CH).astype(F32)
            return carry
        lax.fori_loop(I0, IMG, widen, I0)
        unit = jnp.where(lax.broadcasted_iota(jnp.int32, (CH, CH), I0) == lax.broadcasted_iota(jnp.int32, (CH, CH), I1),
                         ONE, ZERO).astype(BF16)

        def step(i, carry):
            first = (i // QUAD) * IMG + lax.rem(i, QUAD) * PAIR
            px = []
            for q in range(PAIR):
                rows = [xf[pl.ds(first + (q + hb * 192 + wb * SUB), IMG, stride=PIX), :]
                        for hb in range(PAIR) for wb in range(QUAD)]
                px.append(nt_dot(unit, jnp.concatenate(rows, axis=I0).astype(BF16)))
            for g in range(NG):
                store(g, i, jnp.concatenate([p[SUB * g:SUB * g + SUB] for p in px], axis=I0).astype(BF16))
            return carry
        lax.fori_loop(I0, NPAIR, step, I0)

    def col(k, off, n, width):
        piece = cols[k, off:off + n, :]
        return jnp.concatenate([piece] * (width // LANE), axis=I1)

    lane128 = lax.broadcasted_iota(jnp.int32, (SUB, LANE), I1)
    grp = lane128 // IMG

    def halo_copies(src, e):
        up = {'sw': sw, 'sh': jnp.maximum(sh - I1, I0)}
        down = {'sw': sw, 'sh': jnp.minimum(sh + I1, RAD)}
        upx = {'sw': other_w, 'sh': jnp.maximum(sh - I1, I0)}
        downx = {'sw': other_w, 'sh': jnp.minimum(sh + I1, RAD)}

        def cp(s, d, i, dev):
            return pltpu.make_async_remote_copy(
                src_ref=s, dst_ref=d, send_sem=hs_sem.at[e, i], recv_sem=hr_sem.at[e, i],
                device_id=dev, device_id_type=MESH)
        return (
            lambda: cp(src.at[:, TILEH:9, PAIR:TILEH, :, LANE:PXL], ru.at[e], I0, down),
            lambda: cp(src.at[:, RAD:TILEH, PAIR:TILEH, :, I0:LANE], rd.at[e], I1, up),
            lambda: cp(sc.at[e], rc.at[e, RAD:15], PAIR, {'sw': other_w, 'sh': sh}),
            lambda: cp(sc.at[e, 9:PADH], rc.at[e, I0:RAD], RAD, downx),
            lambda: cp(sc.at[e, I0:RAD], rc.at[e, 15:18], QUAD, upx),
        )

    def halo_start(src, e):
        copies = halo_copies(src, e)

        @pl.when(sh < RAD)
        def _():
            copies[I0]().start()

        @pl.when(sh > I0)
        def _():
            copies[I1]().start()
        first = QUAD - PAIR * sw

        def pack(h, carry):
            for half in range(PAIR):
                ls = slice(half * LANE, half * LANE + LANE)
                pieces = []
                for g in range(NG):
                    v = src[g, RAD + h, pl.ds(first, PAIR), :, ls].astype(F32).reshape(QUAD, SUB, LANE)
                    out = jnp.zeros((SUB, LANE), F32)
                    for q in range(QUAD):
                        shift = lax.rem(q * IMG + IMG * (I1 - sw), LANE)
                        out = jnp.where(grp == q, pltpu.roll(v[q], shift, I1), out)
                    pieces.append(out)
                sc[e, TILEH * half + h] = jnp.concatenate(pieces, axis=I0).astype(BF16)
            return carry
        lax.fori_loop(I0, TILEH, pack, I0)
        copies[PAIR]().start()

        @pl.when(sh < RAD)
        def _():
            copies[RAD]().start()

        @pl.when(sh > I0)
        def _():
            copies[QUAD]().start()

        @pl.when(sh == I0)
        def _():
            ru[e] = jnp.zeros(ru.shape[I1:], BF16)
            rc[e, I0:RAD] = jnp.zeros((RAD, CH, LANE), BF16)

        @pl.when(sh == RAD)
        def _():
            rd[e] = jnp.zeros(rd.shape[I1:], BF16)
            rc[e, 15:18] = jnp.zeros((RAD, CH, LANE), BF16)

    def halo_finish(src, e):
        copies = halo_copies(src, e)

        @pl.when(sh < RAD)
        def _():
            copies[I0]().wait_send()
            copies[RAD]().wait_send()
            copies[I1]().wait_recv()
            copies[QUAD]().wait_recv()

        @pl.when(sh > I0)
        def _():
            copies[I1]().wait_send()
            copies[QUAD]().wait_send()
            copies[I0]().wait_recv()
            copies[RAD]().wait_recv()
        copies[PAIR]().wait()
        for r in range(RAD):
            src[:, r, PAIR:TILEH, :, LANE:PXL] = src[:, TILEH + r, PAIR:TILEH, :, I0:LANE]
            src[:, r, PAIR:TILEH, :, I0:LANE] = ru[e, :, r]
            src[:, 9 + r, PAIR:TILEH, :, I0:LANE] = src[:, RAD + r, PAIR:TILEH, :, LANE:PXL]
            src[:, 9 + r, PAIR:TILEH, :, LANE:PXL] = rd[e, :, r]
        is_left = (lane128 < IMG)
        is_right = (lane128 >= TQ)
        keep_left = jnp.where(sw == I1, ONE, ZERO)
        keep_right = jnp.where(sw == I0, ONE, ZERO)

        def pad(h, carry):
            for half in range(PAIR):
                ls = slice(half * LANE, half * LANE + LANE)
                strip = rc[e, h + TILEH * half].astype(F32).reshape(NG, SUB, LANE)
                for g in range(NG):
                    hi = src[g, h, QUAD:TILEH, :, ls].astype(F32).reshape(QUAD, SUB, LANE)
                    lo = src[g, h, PAIR:QUAD, :, ls].astype(F32).reshape(QUAD, SUB, LANE)
                    left, right = [], []
                    for q in range(QUAD):
                        shift = lax.rem(jnp.where(sw == I1, LANE - q * IMG, 224 - q * IMG), LANE)
                        edge = pltpu.roll(strip[g], shift, I1)
                        left.append(jnp.where(is_left, edge * keep_left, pltpu.roll(hi[q], IMG, I1)))
                        right.append(jnp.where(is_right, edge * keep_right, pltpu.roll(lo[q], TQ, I1)))
                    src[g, h, I0:PAIR, :, ls] = jnp.concatenate(left, axis=I0).reshape(PAIR, PR, LANE).astype(BF16)
                    src[g, h, TILEH:SUB, :, ls] = jnp.concatenate(right, axis=I0).reshape(PAIR, PR, LANE).astype(BF16)
            return carry
        lax.fori_loop(I0, PADH, pad, I0)

    def fold(ref):
        v = ref[:, I0:LANE] + ref[:, LANE:PXL]
        v = v + pltpu.roll(v, IMG, I1)
        return v + pltpu.roll(v, HALFL, I1)

    def pack_sums(v):
        gq = lax.broadcasted_iota(jnp.int32, (CH, LANE), I1) // IMG
        out = v[I0:CH]
        for q in range(I1, QUAD):
            out = jnp.where(gq == q, v[CH * q:CH * q + CH], out)
        return out

    def unpack_sums(p):
        gq = lax.broadcasted_iota(jnp.int32, (CH, LANE), I1) // IMG
        rows = []
        for q in range(QUAD):
            z = jnp.where(gq == q, p, ZERO)
            z = z + pltpu.roll(z, IMG, I1)
            rows.append(z + pltpu.roll(z, HALFL, I1))
        return jnp.concatenate(rows, axis=I0)

    def reduce_copies(a):
        return [pltpu.make_async_remote_copy(
            src_ref=sa.at[a], dst_ref=ra.at[a, d - I1], send_sem=as_sem.at[a, d - I1], recv_sem=ar_sem.at[a, d - I1],
            device_id=peer(d), device_id_type=MESH) for d in range(I1, SUB)]

    def reduce_start(a):
        for c in reduce_copies(a):
            c.start()

    def reduce_finish(a):
        for c in reduce_copies(a):
            c.wait()
        total = sa[a]
        for d in range(TAP):
            total = total + ra[a, d]
        return total

    def build_band(way, k):
        diag = lax.rem(lax.broadcasted_iota(jnp.int32, (SUB, LANE), I1), SUB) == lax.broadcasted_iota(jnp.int32, (SUB, LANE), I0)

        def one(g, carry):
            base = jnp.concatenate([jnp.where(diag, jnp.broadcast_to(eb[way, g, i, k:k + I1, :], (SUB, LANE)), ZERO)
                                    for i in range(SUB)], axis=I1)
            for h in range(PAIR):
                for wp in range(QUAD):
                    rows = [pltpu.roll(base, h * LANE + (PAIR * wp + q + I1) * SUB, I1) for q in range(PAIR)]
                    at = (h * QUAD + wp) * PR
                    tbuf[g, at:at + PR, :] = jnp.concatenate(rows, axis=I0).astype(BF16)
            return carry
        lax.fori_loop(I0, NG, one, I0)

    def conv(src, finish):
        def step(hp, carry):
            for g in range(NG):
                tile = src[g, pl.ds(PAIR * hp, SUB)].reshape(BAND, PXL)
                finish(g, hp, dot(tbuf[g], tile))
            return carry
        lax.fori_loop(I0, RAD, step, I0)

    def load_pair(ref, i):
        return [ref[g, i].astype(F32).reshape(PAIR, SUB, PXL) for g in range(NG)]

    def to_mat(pieces):
        return jnp.concatenate([jnp.concatenate([p[q] for p in pieces], axis=I0) for q in range(PAIR)], axis=I1)

    def from_mat(m):
        return [jnp.concatenate([m[SUB * g:SUB * g + SUB, I0:PXL][None], m[SUB * g:SUB * g + SUB, PXL:PXP][None]], axis=I0)
                for g in range(NG)]

    def chan_mean(pieces):
        t = pieces[I0]
        for p in pieces[I1:]:
            t = t + p
        return jnp.sum(t, axis=I1, keepdims=True) * (ONE / 40.0)

    def norm_pair(k, i):
        d = [dbuf[k, g, i].astype(F32).reshape(PAIR, SUB, PXL) for g in range(NG)]
        mu = chan_mean(d)
        c = [v - mu for v in d]
        inv = lax.rsqrt(chan_mean([v * v for v in c]) + EPS)
        return [v * inv for v in c], inv

    def gelu_of(x):
        return (0.5 * x) * (ONE + lax.erf(x * 0.7071067811865476))

    def mask_row(k):
        m = mask[k, I0:I1, :]
        return jnp.concatenate([m, m], axis=I1)

    def conv_forward(k, src):
        bias = [col(k, CONVB + SUB * g, SUB, PXL) for g in range(NG)]

        def finish(g, hp, acc):
            v = acc.reshape(PR, SUB, PXL) + bias[g][None]
            dbuf[k, g, pl.ds(SUB * hp, SUB)] = v.reshape(SUB, PR, PXL).astype(BF16)
        conv(src, finish)

    def hidden_forward(k):
        acc_g2[...] = jnp.zeros_like(acc_g2)

        def step(i, carry):
            nrm, _ = norm_pair(k, i)
            n = [nrm[g] * col(k, NORMG + SUB * g, SUB, PXL)[None] + col(k, NORMB + SUB * g, SUB, PXL)[None] for g in range(NG)]
            n.append(jnp.ones((PAIR, SUB, PXL), F32))
            nb = to_mat(n).astype(BF16)
            nbuf[k, i] = nb
            h = (dot(w1t[k], nb) + col(k, FC1B, HID, PXP)).astype(BF16)
            hbuf[k, i] = h
            g = gelu_of(h.astype(F32))
            g = g * g
            acc_g2[...] += g[:, I0:PXL] + g[:, PXL:PXP]
            return carry
        lax.fori_loop(I0, NPAIR, step, I0)

    def scale_from(k, total):
        gn = jnp.sqrt(unpack_sums(total))
        mean = jnp.sum(gn, axis=I0, keepdims=True) * (ONE / 160.0) + EPS
        gnbuf[k] = gn
        sbuf[k] = cols[k, GAMMA:GAMMA + HID, :] * (gn / mean) + ONE

    def wide(v, width):
        return jnp.concatenate([v] * (width // LANE), axis=I1)

    def resp_of(k, g):
        return (g * wide(sbuf[k], PXP) + col(k, BETA, HID, PXP)).astype(BF16)

    def project(k, i, r, res):
        o = dot(w2t[k], r) + col(k, FC2B, CH, PXP)
        o = from_mat(o * mask_row(k))
        return [(res[g] + o[g]).reshape(PR, PXL).astype(BF16) for g in range(NG)]

    def block1_out():
        def step(i, carry):
            r = resp_of(I0, gelu_of(hbuf[I0, i].astype(F32)))
            hh, wp = i // QUAD, lax.rem(i, QUAD)
            res = [x1[g, RAD + hh, PAIR + wp].astype(F32).reshape(PAIR, SUB, PXL) for g in range(NG)]
            y = project(I0, i, r, res)
            for g in range(NG):
                x2[g, RAD + hh, PAIR + wp] = y[g]
            return carry
        lax.fori_loop(I0, NPAIR, step, I0)

    def cross_phase(k, dy):
        acc_cross[...] = jnp.zeros_like(acc_cross)
        acc_beta[...] = jnp.zeros_like(acc_beta)

        def step(i, carry):
            dm = to_mat(load_pair(dy, i)).astype(BF16)
            dr = (dot(w2[k], dm) * mask_row(k)).astype(BF16)
            drbuf[i] = dr
            dr = dr.astype(F32)
            cr = dr * gelu_of(hbuf[k, i].astype(F32))
            acc_cross[...] += cr[:, I0:PXL] + cr[:, PXL:PXP]
            acc_beta[...] += dr[:, I0:PXL] + dr[:, PXL:PXP]
            return carry
        lax.fori_loop(I0, NPAIR, step, I0)

    def grn_grad(k, total):
        gn = gnbuf[k]
        cross = unpack_sums(total)
        mean = jnp.sum(gn, axis=I0, keepdims=True) * (ONE / 160.0) + EPS
        ds = cols[k, GAMMA:GAMMA + HID, :] * cross
        dg = ds / mean - jnp.sum(ds * gn, axis=I0, keepdims=True) / (mean * mean * 160.0)
        qbuf[...] = dg / gn

    def hidden_backward(k, dy, with_out):
        acc_f1[...] = jnp.zeros_like(acc_f1)
        acc_f2[...] = jnp.zeros_like(acc_f2)
        acc_n[...] = jnp.zeros_like(acc_n)

        def step(i, carry):
            hh, wp = i // QUAD, lax.rem(i, QUAD)
            x = hbuf[k, i].astype(F32)
            phi = 0.5 + 0.5 * lax.erf(x * 0.7071067811865476)
            g = x * phi
            slope = phi + (x * 0.3989422804014327) * jnp.exp(-0.5 * (x * x))
            r = resp_of(k, g)
            if with_out:
                res = [x2[g_, RAD + hh, PAIR + wp].astype(F32).reshape(PAIR, SUB, PXL) for g_ in range(NG)]
                y = project(k, i, r, res)
                for g_ in range(NG):
                    y_out[g_, i] = y[g_]
            dm = to_mat(load_pair(dy, i))
            dz = jnp.where(mask_row(k) > ZERO, dm, ZERO)
            dz = jnp.concatenate([dz, jnp.zeros((SUB, PXP), F32)], axis=I0).astype(BF16)
            nb = nbuf[k, i]
            rhs = jnp.concatenate([nb, dz], axis=I0)
            dga = drbuf[i].astype(F32) * wide(sbuf[k], PXP) + g * wide(qbuf[...], PXP)
            dh = (dga * slope).astype(BF16)
            raug = jnp.concatenate([r, jnp.ones((PR, PXP), BF16)], axis=I0)
            acc_f1[...] += nt_dot(dh, rhs)
            acc_f2[...] += nt_dot(raug, rhs)
            dn = from_mat(dot(w1[k], dh).astype(BF16).astype(F32))
            nrm, inv = norm_pair(k, i)
            dx = [dn[g_] * col(k, NORMG + SUB * g_, SUB, PXL)[None] for g_ in range(NG)]
            m1 = chan_mean(dx)
            m2 = chan_mean([a * b for a, b in zip(dx, nrm)])
            for g_ in range(NG):
                dd = (inv * (dx[g_] - m1 - nrm[g_] * m2)).astype(BF16)
                dp[g_, RAD + hh, PAIR + wp] = dd.reshape(PR, PXL)
                dd = dd.astype(F32)
                pg = dn[g_] * nrm[g_]
                acc_n[I0, SUB * g_:SUB * g_ + SUB, :] += pg[I0] + pg[I1]
                acc_n[I1, SUB * g_:SUB * g_ + SUB, :] += dn[g_][I0] + dn[g_][I1]
                acc_n[PAIR, SUB * g_:SUB * g_ + SUB, :] += dd[I0] + dd[I1]
            return carry
        lax.fori_loop(I0, NPAIR, step, I0)

    def conv_wgrad(k, src):
        sub = lax.broadcasted_iota(jnp.int32, (SUB, BAND), I0)
        lane = lax.rem(lax.broadcasted_iota(jnp.int32, (SUB, BAND), I1), SUB)

        def one(g, carry):
            for hp in range(RAD):
                a = dp[g, RAD + PAIR * hp:NG + PAIR * hp, PAIR:TILEH].reshape(LANE, PXL)
                b = src[g, PAIR * hp:PAIR * hp + SUB].reshape(BAND, PXL)
                part = nt_dot(a, b)
                if hp == I0:
                    gvec[...] = part
                else:
                    gvec[...] += part
            out = jnp.zeros((SUB, BAND), F32)
            for h in range(PAIR):
                for w in range(SUB):
                    at = (h * SUB + w) * SUB
                    out = out + pltpu.roll(gvec[at:at + SUB, :], BAND - (h * LANE + (w + I1) * SUB), I1)
            out = jnp.sum(jnp.where(sub == lane, out, ZERO), axis=I0, keepdims=True)
            rows = jnp.concatenate([out[:, LANE * i:LANE * i + LANE] for i in range(SUB)], axis=I0)
            gb[k, pl.ds(HIDP + SUB * g, SUB), :] = rows
            return carry
        lax.fori_loop(I0, NG, one, I0)

    def store_grads(k):
        lane = lax.broadcasted_iota(jnp.int32, (HIDP, LANE), I1)
        f1 = jnp.concatenate([acc_f1[...], jnp.zeros((PR, TQ), F32)], axis=I0)
        f1 = jnp.concatenate([f1, jnp.zeros((HIDP, IMG), F32)], axis=I1)
        f2 = jnp.concatenate([acc_f2[...], jnp.zeros((HIDP, IMG), F32)], axis=I1)
        out = jnp.where(lane < CHP, f1, jnp.where(lane < CHQ, f2, ZERO))

        def column(v, lane_at, n):
            c = jnp.sum(v, axis=I1, keepdims=True)
            c = jnp.concatenate([c, jnp.zeros((HIDP - n, I1), F32)], axis=I0)
            return jnp.where(lane == lane_at, c, ZERO)
        gn = gnbuf[k]
        mean = jnp.sum(gn, axis=I0, keepdims=True) * (ONE / 160.0) + EPS
        out = out + column(acc_beta[:, I0:LANE] + acc_beta[:, LANE:PXL], CHQ, HID)
        out = out + column((acc_cross[:, I0:LANE] + acc_cross[:, LANE:PXL]) * (gn / mean), 89, HID)
        for j in range(RAD):
            out = out + column(acc_n[j, :, I0:LANE] + acc_n[j, :, LANE:PXL], 90 + j, CH)
        gb[k, I0:HIDP, :] = out
        gb[k, 216:224, :] = jnp.zeros((SUB, LANE), F32)

    def conv_backward(dy, out):
        def finish(g, hp, acc):
            v = acc.reshape(SUB, PR, PXL) + dy[g, pl.ds(SUB * hp, SUB)].astype(F32)
            out[g, pl.ds(SUB * hp, SUB)] = v.astype(BF16)
        conv(dp, finish)

    def to_x1(g, i, v):
        x1[g, RAD + i // QUAD, PAIR + lax.rem(i, QUAD)] = v

    def to_gout(g, i, v):
        gout[g, i] = v
    load_tiles(xin, to_x1)
    halo_start(x1, I0)
    setup()
    load_tiles(gin, to_gout)
    build_band(I0, I0)
    halo_finish(x1, I0)
    conv_forward(I0, x1)
    hidden_forward(I0)
    sa[I0, I0:CH] = pack_sums(fold(acc_g2))
    sa[I0, CH:80] = jnp.zeros((CH, LANE), F32)
    reduce_start(I0)
    build_band(I0, I1)
    total = reduce_finish(I0)
    scale_from(I0, total[I0:CH])
    block1_out()
    halo_start(x2, I1)
    halo_finish(x2, I1)
    conv_forward(I1, x2)
    hidden_forward(I1)
    cross_phase(I1, gout)
    sa[I1, I0:CH] = pack_sums(fold(acc_g2))
    sa[I1, CH:80] = pack_sums(fold(acc_cross))
    reduce_start(I1)
    build_band(I1, I1)
    total = reduce_finish(I1)
    scale_from(I1, total[I0:CH])
    grn_grad(I1, total[CH:80])
    hidden_backward(I1, gout, True)
    halo_start(dp, PAIR)
    conv_wgrad(I1, x2)
    store_grads(I1)
    halo_finish(dp, PAIR)
    conv_backward(gout, dmid)
    cross_phase(I0, dmid)
    sa[PAIR, I0:CH] = pack_sums(fold(acc_cross))
    sa[PAIR, CH:80] = jnp.zeros((CH, LANE), F32)
    reduce_start(PAIR)
    build_band(I1, I0)
    total = reduce_finish(PAIR)
    grn_grad(I0, total[I0:CH])
    hidden_backward(I0, dmid, False)
    halo_start(dp, RAD)
    conv_wgrad(I0, x1)
    store_grads(I0)
    halo_finish(dp, RAD)

    def part(f):
        return gb.at[f // QUAD, pl.ds(pl.multiple_of(lax.rem(f, QUAD) * 56, SUB), 56)]

    scat = [pltpu.make_async_remote_copy(
        src_ref=part(lax.rem(me + d, SUB)), dst_ref=grx.at[d - I1], send_sem=gs_sem.at[d - I1], recv_sem=gr_sem.at[d - I1],
        device_id=peer(d), device_id_type=MESH) for d in range(I1, SUB)]
    for c in scat:
        c.start()
    conv_backward(dmid, dx_out)
    for c in scat:
        c.wait()
    mine = gb[me // QUAD, pl.ds(pl.multiple_of(lax.rem(me, QUAD) * 56, SUB), 56), :]
    for d in range(TAP):
        mine = mine + grx[d]
    gs[TAP] = mine
    gath = [pltpu.make_async_remote_copy(
        src_ref=gs.at[TAP], dst_ref=gs.at[d - I1], send_sem=as2_sem.at[d - I1], recv_sem=ar2_sem.at[d - I1],
        device_id=peer(d), device_id_type=MESH) for d in range(I1, SUB)]
    for c in gath:
        c.start()
    for c in gath:
        c.wait()
    gr_out[me] = gs[TAP]
    for d in range(I1, SUB):
        gr_out[lax.rem(me + SUB - d, SUB)] = gs[d - I1]


def run_kernel(args):
    act = jax.ShapeDtypeStruct((NG, NPAIR, PR, PXL), BF16)
    vm = pl.BlockSpec(memory_space=pltpu.VMEM)
    pad = pltpu.VMEM((NG, PADH, SUB, PR, PXL), BF16)
    return pl.pallas_call(
        kernel,
        name='blocks',
        out_shape=(act, act, jax.ShapeDtypeStruct((SUB, 56, LANE), F32)),
        in_specs=[vm] * len(args),
        out_specs=(vm, vm, vm),
        scratch_shapes=[
            pltpu.VMEM((12288, CH), F32), pltpu.VMEM((NG, NPAIR, PR, PXL), BF16),
            pltpu.VMEM((PAIR, SUB, PXL), F32), pltpu.VMEM((PAIR, NG, SUB, SUB, LANE), F32), pltpu.VMEM((PAIR, 640, LANE), F32),
            pltpu.VMEM((PAIR, HID, CHP), BF16), pltpu.VMEM((PAIR, HID, CH), BF16),
            pad, pad, pad,
            pltpu.VMEM((PAIR, NG, NPAIR, PR, PXL), BF16),
            pltpu.VMEM((PAIR, NPAIR, CHP, PXP), BF16),
            pltpu.VMEM((PAIR, NPAIR, HID, PXP), BF16),
            pltpu.VMEM((NPAIR, HID, PXP), BF16),
            pltpu.VMEM((NG, NPAIR, PR, PXL), BF16),
            pltpu.VMEM((NG, LANE, BAND), BF16),
            pltpu.VMEM((HID, PXL), F32), pltpu.VMEM((HID, PXL), F32), pltpu.VMEM((HID, PXL), F32),
            pltpu.VMEM((RAD, CH, PXL), F32),
            pltpu.VMEM((HID, TQ), F32), pltpu.VMEM((HIDP, TQ), F32),
            pltpu.VMEM((LANE, BAND), F32),
            pltpu.VMEM((PAIR, HID, LANE), F32), pltpu.VMEM((PAIR, HID, LANE), F32), pltpu.VMEM((HID, LANE), F32),
            pltpu.VMEM((QUAD, NG, RAD, QUAD, PR, LANE), BF16), pltpu.VMEM((QUAD, NG, RAD, QUAD, PR, LANE), BF16),
            pltpu.VMEM((QUAD, 18, CH, LANE), BF16), pltpu.VMEM((QUAD, PADH, CH, LANE), BF16),
            pltpu.VMEM((RAD, 80, LANE), F32), pltpu.VMEM((RAD, TAP, 80, LANE), F32),
            pltpu.VMEM((PAIR, ROWS, LANE), F32), pltpu.VMEM((TAP, 56, LANE), F32), pltpu.VMEM((SUB, 56, LANE), F32),
            pltpu.SemaphoreType.DMA((QUAD, NG)), pltpu.SemaphoreType.DMA((QUAD, NG)),
            pltpu.SemaphoreType.DMA((RAD, TAP)), pltpu.SemaphoreType.DMA((RAD, TAP)),
            pltpu.SemaphoreType.DMA((TAP,)), pltpu.SemaphoreType.DMA((TAP,)),
            pltpu.SemaphoreType.DMA((TAP,)), pltpu.SemaphoreType.DMA((TAP,)),
        ],
        compiler_params=pltpu.CompilerParams(collective_id=I0, has_side_effects=True, vmem_limit_bytes=60 * PAIR**20),
    )(*args)


def finish_kernel(y, dx, gr, act_out, grad_in, o_taps, o_bconv, o_gnorm, o_bnorm, o_w1, o_b1, o_gamma, o_beta, o_w2, o_b2, yf):
    def unload(src, dst):
        def step(i, carry):
            first = (i // QUAD) * IMG + lax.rem(i, QUAD) * PAIR
            v = [src[g, i].astype(F32) for g in range(NG)]
            for q in range(PAIR):
                m = jnp.transpose(jnp.concatenate([p[SUB * q:SUB * q + SUB] for p in v], axis=I0))
                for j in range(SUB):
                    yf[pl.ds(first + (q + (j // QUAD) * 192 + (j % QUAD) * SUB), IMG, stride=PIX), :] = m[IMG * j:IMG * j + IMG]
            return carry
        lax.fori_loop(I0, NPAIR, step, I0)

        def narrow(b, carry):
            dst[b] = yf[pl.ds(pl.multiple_of(b * PIX, PIX), PIX), :].reshape(PADH, IMG, CH).astype(BF16)
            return carry
        lax.fori_loop(I0, IMG, narrow, I0)
    unload(y, act_out)
    unload(dx, grad_in)
    for k in range(PAIR):
        t = jnp.transpose(gr[k, I0:HID, :])
        o_w1[k] = t[I0:CH]
        o_w2[k] = t[CHP:CHQ] * KEEP
        o_b1[k:k + I1, :] = t[CH:41]
        o_beta[k:k + I1, :] = t[CHQ:89]
        o_gamma[k:k + I1, :] = t[89:90]
        o_gnorm[k:k + I1, :] = t[90:91, I0:CH]
        o_bnorm[k:k + I1, :] = t[91:92, I0:CH]
        o_bconv[k:k + I1, :] = t[92:93, I0:CH]
        o_b2[k:k + I1, :] = gr[k, HID:161, CHP:CHQ] * KEEP
    place = lax.broadcasted_iota(jnp.int32, (PAIR, LANE), I1) // SUB

    def taps_row(i, carry):
        for j in range(TAP):
            out = jnp.zeros((PAIR, LANE), F32)
            for g in range(NG):
                rows = jnp.concatenate([gr[k, pl.ds(HIDP + SUB * g + i, I1), :] for k in range(PAIR)], axis=I0)
                out = jnp.where(place == g, pltpu.roll(rows, (LANE + SUB * (g - j)) % LANE, I1), out)
            o_taps[i, j] = out[:, I0:CH]
        return carry
    lax.fori_loop(I0, TAP, taps_row, I0)


def finish(y, dx, gr):
    vm = pl.BlockSpec(memory_space=pltpu.VMEM)
    shape = lambda *s: jax.ShapeDtypeStruct(s, F32)
    act = jax.ShapeDtypeStruct((IMG, PADH, IMG, CH), BF16)
    small, wide = shape(PAIR, CH), shape(PAIR, HID)
    return pl.pallas_call(
        finish_kernel, name='finish',
        out_shape=(act, act, shape(TAP, TAP, PAIR, CH), small, small, small, shape(PAIR, CH, HID), wide, wide, wide, shape(PAIR, CH, HID), small),
        in_specs=[vm] * RAD, out_specs=(vm,) * PADH,
        scratch_shapes=[pltpu.VMEM((12288, CH), F32)],
        compiler_params=pltpu.CompilerParams(vmem_limit_bytes=CH * PAIR**20),
    )(y, dx, gr)


def solution(mesh):
    act_spec = P('dp', 'sh', 'sw', None)
    rep = P()

    def local_step(act_in, drop_mask, grad_out, conv_w, conv_b, norm_g, norm_b, fc1_w, fc1_b, grn_gamma, grn_beta, fc2_w, fc2_b):
        y, dx, gr = run_kernel((act_in, grad_out, drop_mask.T, conv_w.transpose(I1, PAIR, I0, RAD), fc1_b, grn_gamma, grn_beta,
                                conv_b, norm_g, norm_b, fc2_b, fc1_w, fc2_w.transpose(I0, PAIR, I1)))
        act_out, grad_in, taps, *rest = finish(y, dx, gr.reshape(PAIR, ROWS, LANE))
        rest[TAP] = rest[TAP].transpose(I0, PAIR, I1)
        return (act_out, grad_in, taps.transpose(PAIR, I0, I1, RAD), *rest)

    return jax.shard_map(local_step, mesh=mesh,
                         in_specs=(act_spec, P('dp', None), act_spec) + (rep,) * 10,
                         out_specs=(act_spec, act_spec) + (P('dp'),) * 10,
                         check_vma=False)
```

time: 630 us -> 157 us (0.25)
  matrix products: 304 us -> 0 us
  Pallas kernels: 0 us -> 152 us
  blocking collectives: 94.5 us -> 0 us
  other arithmetic: 93 us -> 0 us
  starting transfers between devices: 45 us -> 0 us
  local copies, waits for them, and re-layouts: 42.4 us -> 3.33 us
  waiting for transfers between devices: 29.9 us -> 0 us
  between operations: 15.8 us -> 0.67 us
    conv_general_dilated x6 -> x0, matrix products: 183 us -> none  [the longest x4 113 us: depthwise(): lax.conv_general_dilated(padded, kernel[:, :, None, :], (1, 1), 'VALID',...]
    pallas_call x0 -> x2, Pallas kernels: none -> 152 us  [the longest x1 135 us: run_kernel(): pl.pallas_call(kernel, name='blocks', out_shape=(act, act, jax.ShapeDtype...]
    dot_general x16 -> x0, matrix products: 122 us -> none  [the longest x2 45.5 us: block_backward(): jnp.einsum('bhwc,kc->bhwk', d_out, fc2_w, preferred_element_type=jnp.floa...]
    psum x3 -> x0, blocking collectives: 94.5 us -> none  [the longest x2 64.3 us: block_forward(): lax.psum(jnp.sum(g_act * g_act, axis=(1, 2)), ('sh', 'sw'))]
    reduce_sum x10 -> x0, other arithmetic: 56 us -> none  [the longest x2 27.8 us: block_backward(): grad_fc1_b = jnp.sum(d_hidden, axis=(0, 1, 2), dtype=jnp.float32)]
    ppermute x16 -> x0, starting transfers between devices: 45 us -> none  [shift_from(): return lax.ppermute(strip, axis_name, perm_pairs)]
    unnamed x201 -> x6, local copies, waits for them, and re-layouts: 25.1 us -> 3.33 us
    convert_element_type x3 -> x0, other arithmetic: 16.8 us -> none  [the longest x1 8.69 us: block_forward(): (grn_gamma * (g_act * grn_scale[:, None, None, :]) + grn_beta + g_act).as...]
  transfers between devices with their start and end apart: 17 -> 0, of which waited for: 7 -> 0; matrix products, arithmetic and copies ran while one was open for 16% -> 0% of each run, Pallas kernels for 0% -> 0%
where the time goes in v1:
time: 157 us; the launch traced here: 156 us
  Pallas kernels  152 us (97%)
  local copies, waits for them, and re-layouts  3.33 us (2%)
    pallas_call x1, Pallas kernels, run_kernel(): pl.pallas_call(kernel, name='blocks', out_shape=(act, act, jax.ShapeDtype...  135 us
    pallas_call x1, Pallas kernels, finish(): pl.pallas_call(finish_kernel, name='finish', out_shape=(act, act, shape(T...  17.8 us
    unnamed x6, local copies, waits for them, and re-layouts  3.33 us

profile of v1, /device:TPU:0, one launch (start us, length us, event | category | flops | bytes accessed | tf_op | source)
XLA Modules:
  0.0 156.3 jit_solution(5441897312787004886)
XLA Ops:
  0.6 134.5 %blocks.1 = (bf16[5,24,16,256]{3,2,1,0:T(8,128)(2,1)}, bf16[5,24,16,256]{3,2,1,0:T(8,128)(2,1)}, f32[8,56,128]{2,1,0:T(8,128)}) custom-call(bf16[32,12,32,40]{3,2,1,0:T(8,128)(2,1)} %xin.1, bf16[32,12,32,40]{3,2,1,0:T(8,128)(2,1)} %gin.1, f32[2,32]{1,0:T(2,128)} %bitcast.9, bf16[7,7,2,40]{3,2,1,0:T(2,128)(2,1)} %bitcast.8, f32[2,160]{1,0:T(2,128)} %b_fc1.1, ...), custom_call_target="tpu_custom_call" | custom-call | tf_op jit(solution)/shard_map/blocks/pallas_call | solution.py:582
  135.2 0.0 copy-start
  135.2 1.2 copy-done
  136.4 0.0 copy-start.1
  136.4 1.2 copy-done.1
  137.6 0.0 copy-start.2
  137.6 0.9 copy-done.2
  138.5 17.8 %finish.1 = (bf16[32,12,32,40]{3,2,1,0:T(8,128)(2,1)}, bf16[32,12,32,40]{3,2,1,0:T(8,128)(2,1)}, f32[7,7,2,40]{3,2,1,0:T(2,128)}, f32[2,40]{1,0:T(2,128)}, f32[2...) custom-call(bf16[5,24,16,256]{3,2,1,0:T(8,128)(2,1)S(1)} %copy-done,, ...), custom_call_target="tpu_custom_call" | custom-call | tf_op jit(solution)/shard_map/finish/pallas_call | solution.py:664
Async XLA Ops:
  135.2 1.2 copy-start
  136.4 1.2 copy-start.1
  137.6 0.9 copy-start.2

commit v2 on v1

--- a/solution.py
+++ b/solution.py
@@ -104,9 +104,9 @@
 
     def load_tiles(src, store):
         def widen(b, carry):
-            xf[pl.ds(pl.multiple_of(b * PIX, PIX), PIX), :] = src[b].reshape(PIX, CH).astype(F32)
-            return carry
-        lax.fori_loop(I0, IMG, widen, I0)
+            xf[pl.ds(b * 385, PIX), :] = src[b].reshape(PIX, CH).astype(F32)
+            return carry
+        lax.fori_loop(I0, IMG, widen, I0, unroll=QUAD)
         unit = jnp.where(lax.broadcasted_iota(jnp.int32, (CH, CH), I0) == lax.broadcasted_iota(jnp.int32, (CH, CH), I1),
                          ONE, ZERO).astype(BF16)
 
@@ -114,13 +114,13 @@
             first = (i // QUAD) * IMG + lax.rem(i, QUAD) * PAIR
             px = []
             for q in range(PAIR):
-                rows = [xf[pl.ds(first + (q + hb * 192 + wb * SUB), IMG, stride=PIX), :]
+                rows = [xf[pl.ds(first + (q + hb * 192 + wb * SUB), IMG, stride=385), :]
                         for hb in range(PAIR) for wb in range(QUAD)]
                 px.append(nt_dot(unit, jnp.concatenate(rows, axis=I0).astype(BF16)))
             for g in range(NG):
                 store(g, i, jnp.concatenate([p[SUB * g:SUB * g + SUB] for p in px], axis=I0).astype(BF16))
             return carry
-        lax.fori_loop(I0, NPAIR, step, I0)
+        lax.fori_loop(I0, NPAIR, step, I0, unroll=QUAD)
 
     def col(k, off, n, width):
         piece = cols[k, off:off + n, :]
@@ -172,7 +172,7 @@
                     pieces.append(out)
                 sc[e, TILEH * half + h] = jnp.concatenate(pieces, axis=I0).astype(BF16)
             return carry
-        lax.fori_loop(I0, TILEH, pack, I0)
+        lax.fori_loop(I0, TILEH, pack, I0, unroll=PAIR)
         copies[PAIR]().start()
 
         @pl.when(sh < RAD)
@@ -236,7 +236,7 @@
                     src[g, h, I0:PAIR, :, ls] = jnp.concatenate(left, axis=I0).reshape(PAIR, PR, LANE).astype(BF16)
                     src[g, h, TILEH:SUB, :, ls] = jnp.concatenate(right, axis=I0).reshape(PAIR, PR, LANE).astype(BF16)
             return carry
-        lax.fori_loop(I0, PADH, pad, I0)
+        lax.fori_loop(I0, PADH, pad, I0, unroll=PAIR)
 
     def fold(ref):
         v = ref[:, I0:LANE] + ref[:, LANE:PXL]
@@ -259,21 +259,21 @@
             rows.append(z + pltpu.roll(z, HALFL, I1))
         return jnp.concatenate(rows, axis=I0)
 
-    def reduce_copies(a):
+    def reduce_copies(a, n):
         return [pltpu.make_async_remote_copy(
-            src_ref=sa.at[a], dst_ref=ra.at[a, d - I1], send_sem=as_sem.at[a, d - I1], recv_sem=ar_sem.at[a, d - I1],
+            src_ref=sa.at[a, I0:n], dst_ref=ra.at[a, d - I1, I0:n], send_sem=as_sem.at[a, d - I1], recv_sem=ar_sem.at[a, d - I1],
             device_id=peer(d), device_id_type=MESH) for d in range(I1, SUB)]
 
-    def reduce_start(a):
-        for c in reduce_copies(a):
+    def reduce_start(a, n):
+        for c in reduce_copies(a, n):
             c.start()
 
-    def reduce_finish(a):
-        for c in reduce_copies(a):
+    def reduce_finish(a, n):
+        for c in reduce_copies(a, n):
             c.wait()
-        total = sa[a]
+        total = sa[a, I0:n]
         for d in range(TAP):
-            total = total + ra[a, d]
+            total = total + ra[a, d, I0:n]
         return total
 
     def build_band(way, k):
@@ -288,7 +288,7 @@
                     at = (h * QUAD + wp) * PR
                     tbuf[g, at:at + PR, :] = jnp.concatenate(rows, axis=I0).astype(BF16)
             return carry
-        lax.fori_loop(I0, NG, one, I0)
+        lax.fori_loop(I0, NG, one, I0, unroll=NG)
 
     def conv(src, finish):
         def step(hp, carry):
@@ -296,7 +296,7 @@
                 tile = src[g, pl.ds(PAIR * hp, SUB)].reshape(BAND, PXL)
                 finish(g, hp, dot(tbuf[g], tile))
             return carry
-        lax.fori_loop(I0, RAD, step, I0)
+        lax.fori_loop(I0, RAD, step, I0, unroll=RAD)
 
     def load_pair(ref, i):
         return [ref[g, i].astype(F32).reshape(PAIR, SUB, PXL) for g in range(NG)]
@@ -336,8 +336,10 @@
             dbuf[k, g, pl.ds(SUB * hp, SUB)] = v.reshape(SUB, PR, PXL).astype(BF16)
         conv(src, finish)
 
-    def hidden_forward(k):
+    def hidden_forward(k, with_cross):
         acc_g2[...] = jnp.zeros_like(acc_g2)
+        if with_cross:
+            acc_cross[...] = jnp.zeros_like(acc_cross)
 
         def step(i, carry):
             nrm, _ = norm_pair(k, i)
@@ -348,10 +350,13 @@
             h = (dot(w1t[k], nb) + col(k, FC1B, HID, PXP)).astype(BF16)
             hbuf[k, i] = h
             g = gelu_of(h.astype(F32))
+            if with_cross:
+                cr = drbuf[i].astype(F32) * g
+                acc_cross[...] += cr[:, I0:PXL] + cr[:, PXL:PXP]
             g = g * g
             acc_g2[...] += g[:, I0:PXL] + g[:, PXL:PXP]
             return carry
-        lax.fori_loop(I0, NPAIR, step, I0)
+        lax.fori_loop(I0, NPAIR, step, I0, unroll=QUAD)
 
     def scale_from(k, total):
         gn = jnp.sqrt(unpack_sums(total))
@@ -379,10 +384,11 @@
             for g in range(NG):
                 x2[g, RAD + hh, PAIR + wp] = y[g]
             return carry
-        lax.fori_loop(I0, NPAIR, step, I0)
-
-    def cross_phase(k, dy):
-        acc_cross[...] = jnp.zeros_like(acc_cross)
+        lax.fori_loop(I0, NPAIR, step, I0, unroll=QUAD)
+
+    def resp_phase(k, dy, with_cross):
+        if with_cross:
+            acc_cross[...] = jnp.zeros_like(acc_cross)
         acc_beta[...] = jnp.zeros_like(acc_beta)
 
         def step(i, carry):
@@ -390,11 +396,12 @@
             dr = (dot(w2[k], dm) * mask_row(k)).astype(BF16)
             drbuf[i] = dr
             dr = dr.astype(F32)
-            cr = dr * gelu_of(hbuf[k, i].astype(F32))
-            acc_cross[...] += cr[:, I0:PXL] + cr[:, PXL:PXP]
+            if with_cross:
+                cr = dr * gelu_of(hbuf[k, i].astype(F32))
+                acc_cross[...] += cr[:, I0:PXL] + cr[:, PXL:PXP]
             acc_beta[...] += dr[:, I0:PXL] + dr[:, PXL:PXP]
             return carry
-        lax.fori_loop(I0, NPAIR, step, I0)
+        lax.fori_loop(I0, NPAIR, step, I0, unroll=QUAD)
 
     def grn_grad(k, total):
         gn = gnbuf[k]
@@ -445,7 +452,7 @@
                 acc_n[I1, SUB * g_:SUB * g_ + SUB, :] += dn[g_][I0] + dn[g_][I1]
                 acc_n[PAIR, SUB * g_:SUB * g_ + SUB, :] += dd[I0] + dd[I1]
             return carry
-        lax.fori_loop(I0, NPAIR, step, I0)
+        lax.fori_loop(I0, NPAIR, step, I0, unroll=QUAD)
 
     def conv_wgrad(k, src):
         sub = lax.broadcasted_iota(jnp.int32, (SUB, BAND), I0)
@@ -469,7 +476,7 @@
             rows = jnp.concatenate([out[:, LANE * i:LANE * i + LANE] for i in range(SUB)], axis=I0)
             gb[k, pl.ds(HIDP + SUB * g, SUB), :] = rows
             return carry
-        lax.fori_loop(I0, NG, one, I0)
+        lax.fori_loop(I0, NG, one, I0, unroll=NG)
 
     def store_grads(k):
         lane = lax.broadcasted_iota(jnp.int32, (HIDP, LANE), I1)
@@ -505,28 +512,27 @@
     load_tiles(xin, to_x1)
     halo_start(x1, I0)
     setup()
-    load_tiles(gin, to_gout)
     build_band(I0, I0)
     halo_finish(x1, I0)
     conv_forward(I0, x1)
-    hidden_forward(I0)
+    hidden_forward(I0, False)
     sa[I0, I0:CH] = pack_sums(fold(acc_g2))
-    sa[I0, CH:80] = jnp.zeros((CH, LANE), F32)
-    reduce_start(I0)
+    reduce_start(I0, CH)
+    load_tiles(gin, to_gout)
     build_band(I0, I1)
-    total = reduce_finish(I0)
-    scale_from(I0, total[I0:CH])
+    total = reduce_finish(I0, CH)
+    scale_from(I0, total)
     block1_out()
     halo_start(x2, I1)
+    resp_phase(I1, gout, False)
     halo_finish(x2, I1)
     conv_forward(I1, x2)
-    hidden_forward(I1)
-    cross_phase(I1, gout)
+    hidden_forward(I1, True)
     sa[I1, I0:CH] = pack_sums(fold(acc_g2))
     sa[I1, CH:80] = pack_sums(fold(acc_cross))
-    reduce_start(I1)
+    reduce_start(I1, 80)
     build_band(I1, I1)
-    total = reduce_finish(I1)
+    total = reduce_finish(I1, 80)
     scale_from(I1, total[I0:CH])
     grn_grad(I1, total[CH:80])
     hidden_backward(I1, gout, True)
@@ -535,18 +541,16 @@
     store_grads(I1)
     halo_finish(dp, PAIR)
     conv_backward(gout, dmid)
-    cross_phase(I0, dmid)
+    resp_phase(I0, dmid, True)
     sa[PAIR, I0:CH] = pack_sums(fold(acc_cross))
-    sa[PAIR, CH:80] = jnp.zeros((CH, LANE), F32)
-    reduce_start(PAIR)
+    reduce_start(PAIR, CH)
     build_band(I1, I0)
-    total = reduce_finish(PAIR)
-    grn_grad(I0, total[I0:CH])
+    total = reduce_finish(PAIR, CH)
+    grn_grad(I0, total)
     hidden_backward(I0, dmid, False)
     halo_start(dp, RAD)
     conv_wgrad(I0, x1)
     store_grads(I0)
-    halo_finish(dp, RAD)
 
     def part(f):
         return gb.at[f // QUAD, pl.ds(pl.multiple_of(lax.rem(f, QUAD) * 56, SUB), 56)]
@@ -556,6 +560,7 @@
         device_id=peer(d), device_id_type=MESH) for d in range(I1, SUB)]
     for c in scat:
         c.start()
+    halo_finish(dp, RAD)
     conv_backward(dmid, dx_out)
     for c in scat:
         c.wait()
@@ -586,7 +591,7 @@
         in_specs=[vm] * len(args),
         out_specs=(vm, vm, vm),
         scratch_shapes=[
-            pltpu.VMEM((12288, CH), F32), pltpu.VMEM((NG, NPAIR, PR, PXL), BF16),
+            pltpu.VMEM((IMG * 385, CH), F32), pltpu.VMEM((NG, NPAIR, PR, PXL), BF16),
             pltpu.VMEM((PAIR, SUB, PXL), F32), pltpu.VMEM((PAIR, NG, SUB, SUB, LANE), F32), pltpu.VMEM((PAIR, 640, LANE), F32),
             pltpu.VMEM((PAIR, HID, CHP), BF16), pltpu.VMEM((PAIR, HID, CH), BF16),
             pad, pad, pad,
@@ -615,58 +620,61 @@
 
 
 def finish_kernel(y, dx, gr, act_out, grad_in, o_taps, o_bconv, o_gnorm, o_bnorm, o_w1, o_b1, o_gamma, o_beta, o_w2, o_b2, yf):
-    def unload(src, dst):
-        def step(i, carry):
-            first = (i // QUAD) * IMG + lax.rem(i, QUAD) * PAIR
-            v = [src[g, i].astype(F32) for g in range(NG)]
+    def unload(src, dst, n):
+        for wp in range(QUAD):
+            v = [src[g, wp].astype(F32) for g in range(NG)]
             for q in range(PAIR):
                 m = jnp.transpose(jnp.concatenate([p[SUB * q:SUB * q + SUB] for p in v], axis=I0))
                 for j in range(SUB):
-                    yf[pl.ds(first + (q + (j // QUAD) * 192 + (j % QUAD) * SUB), IMG, stride=PIX), :] = m[IMG * j:IMG * j + IMG]
-            return carry
-        lax.fori_loop(I0, NPAIR, step, I0)
-
-        def narrow(b, carry):
-            dst[b] = yf[pl.ds(pl.multiple_of(b * PIX, PIX), PIX), :].reshape(PADH, IMG, CH).astype(BF16)
-            return carry
-        lax.fori_loop(I0, IMG, narrow, I0)
-    unload(y, act_out)
-    unload(dx, grad_in)
-    for k in range(PAIR):
-        t = jnp.transpose(gr[k, I0:HID, :])
-        o_w1[k] = t[I0:CH]
-        o_w2[k] = t[CHP:CHQ] * KEEP
-        o_b1[k:k + I1, :] = t[CH:41]
-        o_beta[k:k + I1, :] = t[CHQ:89]
-        o_gamma[k:k + I1, :] = t[89:90]
-        o_gnorm[k:k + I1, :] = t[90:91, I0:CH]
-        o_bnorm[k:k + I1, :] = t[91:92, I0:CH]
-        o_bconv[k:k + I1, :] = t[92:93, I0:CH]
-        o_b2[k:k + I1, :] = gr[k, HID:161, CHP:CHQ] * KEEP
-    place = lax.broadcasted_iota(jnp.int32, (PAIR, LANE), I1) // SUB
-
-    def taps_row(i, carry):
-        for j in range(TAP):
-            out = jnp.zeros((PAIR, LANE), F32)
-            for g in range(NG):
-                rows = jnp.concatenate([gr[k, pl.ds(HIDP + SUB * g + i, I1), :] for k in range(PAIR)], axis=I0)
-                out = jnp.where(place == g, pltpu.roll(rows, (LANE + SUB * (g - j)) % LANE, I1), out)
-            o_taps[i, j] = out[:, I0:CH]
-        return carry
-    lax.fori_loop(I0, TAP, taps_row, I0)
+                    at = (j // QUAD) * 1056 + (j % QUAD) * SUB + PAIR * wp + q
+                    yf[n, pl.ds(at, IMG, stride=33), :] = m[IMG * j:IMG * j + IMG]
+        for hb in range(PAIR):
+            for b in range(IMG):
+                at = hb * 1056 + b * 33
+                dst[b, hb, I0] = yf[n, at:at + IMG, :].astype(BF16)
+    unload(y, act_out, I0)
+    unload(dx, grad_in, I1)
+
+    @pl.when(pl.program_id(I0) == I0)
+    def _():
+        for k in range(PAIR):
+            t = jnp.transpose(gr[k, I0:HID, :])
+            o_w1[k] = t[I0:CH]
+            o_w2[k] = t[CHP:CHQ] * KEEP
+            o_b1[k:k + I1, :] = t[CH:41]
+            o_beta[k:k + I1, :] = t[CHQ:89]
+            o_gamma[k:k + I1, :] = t[89:90]
+            o_gnorm[k:k + I1, :] = t[90:91, I0:CH]
+            o_bnorm[k:k + I1, :] = t[91:92, I0:CH]
+            o_bconv[k:k + I1, :] = t[92:93, I0:CH]
+            o_b2[k:k + I1, :] = gr[k, HID:161, CHP:CHQ] * KEEP
+        place = lax.broadcasted_iota(jnp.int32, (PAIR, LANE), I1) // SUB
+
+        def taps_row(i, carry):
+            for j in range(TAP):
+                out = jnp.zeros((PAIR, LANE), F32)
+                for g in range(NG):
+                    rows = jnp.concatenate([gr[k, pl.ds(HIDP + SUB * g + i, I1), :] for k in range(PAIR)], axis=I0)
+                    out = jnp.where(place == g, pltpu.roll(rows, (LANE + SUB * (g - j)) % LANE, I1), out)
+                o_taps[i, j] = out[:, I0:CH]
+            return carry
+        lax.fori_loop(I0, TAP, taps_row, I0)
 
 
 def finish(y, dx, gr):
-    vm = pl.BlockSpec(memory_space=pltpu.VMEM)
-    shape = lambda *s: jax.ShapeDtypeStruct(s, F32)
-    act = jax.ShapeDtypeStruct((IMG, PADH, IMG, CH), BF16)
+    shape = lambda *d: jax.ShapeDtypeStruct(d, F32)
+    act = jax.ShapeDtypeStruct((IMG, PAIR, TILEH, IMG, CH), BF16)
     small, wide = shape(PAIR, CH), shape(PAIR, HID)
+    tile = pl.BlockSpec((NG, QUAD, PR, PXL), lambda h: (I0, h, I0, I0))
+    rows = pl.BlockSpec((IMG, PAIR, I1, IMG, CH), lambda h: (I0, I0, h, I0, I0))
+    whole = lambda o: pl.BlockSpec(o.shape, lambda h: (I0,) * len(o.shape))
+    grads = (shape(TAP, TAP, PAIR, CH), small, small, small, shape(PAIR, CH, HID), wide, wide, wide, shape(PAIR, CH, HID), small)
     return pl.pallas_call(
-        finish_kernel, name='finish',
-        out_shape=(act, act, shape(TAP, TAP, PAIR, CH), small, small, small, shape(PAIR, CH, HID), wide, wide, wide, shape(PAIR, CH, HID), small),
-        in_specs=[vm] * RAD, out_specs=(vm,) * PADH,
-        scratch_shapes=[pltpu.VMEM((12288, CH), F32)],
-        compiler_params=pltpu.CompilerParams(vmem_limit_bytes=CH * PAIR**20),
+        finish_kernel, name='finish', grid=(TILEH,),
+        out_shape=(act, act) + grads,
+        in_specs=[tile, tile, whole(gr)], out_specs=(rows, rows) + tuple(whole(o) for o in grads),
+        scratch_shapes=[pltpu.VMEM((PAIR, 2112, CH), F32)],
+        compiler_params=pltpu.CompilerParams(vmem_limit_bytes=60 * PAIR**20),
     )(y, dx, gr)
 
 
@@ -679,7 +687,7 @@
                                 conv_b, norm_g, norm_b, fc2_b, fc1_w, fc2_w.transpose(I0, PAIR, I1)))
         act_out, grad_in, taps, *rest = finish(y, dx, gr.reshape(PAIR, ROWS, LANE))
         rest[TAP] = rest[TAP].transpose(I0, PAIR, I1)
-        return (act_out, grad_in, taps.transpose(PAIR, I0, I1, RAD), *rest)
+        return (act_out.reshape(IMG, PADH, IMG, CH), grad_in.reshape(IMG, PADH, IMG, CH), taps.transpose(PAIR, I0, I1, RAD), *rest)
 
     return jax.shard_map(local_step, mesh=mesh,
                          in_specs=(act_spec, P('dp', None), act_spec) + (rep,) * 10,

time: 157 us -> 106 us (0.68)
  Pallas kernels: 152 us -> 105 us
  local copies, waits for them, and re-layouts: 3.33 us -> 0 us
    pallas_call x1, Pallas kernels: 135 us -> 97.3 us  [run_kernel(): pl.pallas_call(kernel, name='blocks', out_shape=(act, act, jax.ShapeDtype...]
    pallas_call x1, Pallas kernels: 17.8 us -> 7.97 us  [finish(): pl.pallas_call(finish_kernel, name='finish', grid=(TILEH,), out_shape=(ac...]
    unnamed x6 -> x0, local copies, waits for them, and re-layouts: 3.33 us -> none
where the time goes in v2:
time: 106 us
  Pallas kernels  105 us (99%)
    pallas_call x1, Pallas kernels, run_kernel(): pl.pallas_call(kernel, name='blocks', out_shape=(act, act, jax.ShapeDtype...  97.3 us
    pallas_call x1, Pallas kernels, finish(): pl.pallas_call(finish_kernel, name='finish', grid=(TILEH,), out_shape=(ac...  7.97 us

profile of v2, /device:TPU:0, one launch (start us, length us, event | category | flops | bytes accessed | tf_op | source)
XLA Modules:
  0.0 106.1 jit_solution(9501524742690310581)
XLA Ops:
  0.6 97.3 %blocks.1 = (bf16[5,24,16,256]{3,2,1,0:T(8,128)(2,1)}, bf16[5,24,16,256]{3,2,1,0:T(8,128)(2,1)}, f32[8,56,128]{2,1,0:T(8,128)}) custom-call(bf16[32,12,32,40]{3,2,1,0:T(8,128)(2,1)} %xin.1, bf16[32,12,32,40]{3,2,1,0:T(8,128)(2,1)} %gin.1, f32[2,32]{1,0:T(2,128)} %bitcast.11, bf16[7,7,2,40]{3,2,1,0:T(2,128)(2,1)} %bitcast.10, f32[2,160]{1,0:T(2,128)} %b_fc1.1, ...), custom_call_target="tpu_custom_call" | custom-call | tf_op jit(solution)/shard_map/blocks/pallas_call | solution.py:587
  97.9 8.0 %finish.1 = (bf16[32,2,6,32,40]{4,3,2,1,0:T(8,128)(2,1)}, bf16[32,2,6,32,40]{4,3,2,1,0:T(8,128)(2,1)}, f32[7,7,2,40]{3,2,1,0:T(2,128)}, f32[2,40]{1,0:T(2,128)},...) custom-call(bf16[5,24,16,256]{3,2,1,0:T(8,128)(2,1)} %get-tuple-elem, ...), custom_call_target="tpu_custom_call" | custom-call | tf_op jit(solution)/shard_map/finish/pallas_call | solution.py:672

commit v3 on v2

--- a/solution.py
+++ b/solution.py
@@ -30,7 +30,6 @@
 TQ = 96
 CHP = 48
 BAND = 1024
-PIX = 384
 HIDP = 176
 CHQ = 88
 HALFL = 64
@@ -55,11 +54,11 @@
 
 
 def kernel(xin, gin, mask_in, taps, b_fc1, gamma, beta, b_conv, g_norm, b_norm, b_fc2, w1, w2t,
-           y_out, dx_out, gr_out,
-           xf, gout, mask, eb, cols, w1t, w2, x1, x2, dp, dbuf, nbuf, hbuf, drbuf, dmid, tbuf,
+           act_out, grad_in, o_taps, o_bconv, o_gnorm, o_bnorm, o_w1, o_b1, o_gamma, o_beta, o_w2, o_b2,
+           io, xf, gout, ytile, mask, eb, cols, w1t, w2, x1, x2, dp, dbuf, nbuf, hbuf, g0buf, slbuf, drbuf, dmid, tbuf,
            acc_g2, acc_cross, acc_beta, acc_n, acc_f1, acc_f2, gvec, sbuf, gnbuf, qbuf,
-           ru, rd, rc, sc, sa, ra, gb, grx, gs,
-           hs_sem, hr_sem, as_sem, ar_sem, gs_sem, gr_sem, as2_sem, ar2_sem):
+           ru, rd, rc, sc, sa, ra, gb, grx, gs, grf,
+           io_sem, hs_sem, hr_sem, as_sem, ar_sem, gs_sem, gr_sem, as2_sem, ar2_sem):
     sw = lax.axis_index('sw')
     sh = lax.axis_index('sh')
     me = sw * QUAD + sh
@@ -72,7 +71,6 @@
     barrier = pltpu.get_barrier_semaphore()
     for d in range(I1, SUB):
         pl.semaphore_signal(barrier, inc=I1, device_id=peer(d), device_id_type=MESH)
-    pl.semaphore_wait(barrier, TAP)
 
     def setup():
         spots = ((b_fc1, FC1B), (gamma, GAMMA), (beta, BETA), (b_conv, CONVB),
@@ -102,25 +100,53 @@
             return carry
         lax.fori_loop(I0, TAP, taps_row, I0)
 
-    def load_tiles(src, store):
-        def widen(b, carry):
-            xf[pl.ds(b * 385, PIX), :] = src[b].reshape(PIX, CH).astype(F32)
-            return carry
-        lax.fori_loop(I0, IMG, widen, I0, unroll=QUAD)
+    def fetch(src, c):
+        return pltpu.make_async_copy(src.at[SUB * c:SUB * c + SUB], io.at[SUB * c:SUB * c + SUB], io_sem.at[c])
+
+    def load_tiles(store):
         unit = jnp.where(lax.broadcasted_iota(jnp.int32, (CH, CH), I0) == lax.broadcasted_iota(jnp.int32, (CH, CH), I1),
                          ONE, ZERO).astype(BF16)
 
-        def step(i, carry):
-            first = (i // QUAD) * IMG + lax.rem(i, QUAD) * PAIR
-            px = []
-            for q in range(PAIR):
-                rows = [xf[pl.ds(first + (q + hb * 192 + wb * SUB), IMG, stride=385), :]
-                        for hb in range(PAIR) for wb in range(QUAD)]
-                px.append(nt_dot(unit, jnp.concatenate(rows, axis=I0).astype(BF16)))
-            for g in range(NG):
-                store(g, i, jnp.concatenate([p[SUB * g:SUB * g + SUB] for p in px], axis=I0).astype(BF16))
-            return carry
-        lax.fori_loop(I0, NPAIR, step, I0, unroll=QUAD)
+        def step(h, carry):
+            for hb in range(PAIR):
+                for b in range(IMG):
+                    at = hb * 1056 + b * 33
+                    xf[at:at + IMG, :] = io[b, hb * TILEH + h].astype(F32)
+            for wp in range(QUAD):
+                px = []
+                for q in range(PAIR):
+                    rows = [xf[pl.ds(hb * 1056 + wb * SUB + PAIR * wp + q, IMG, stride=33), :]
+                            for hb in range(PAIR) for wb in range(QUAD)]
+                    px.append(nt_dot(unit, jnp.concatenate(rows, axis=I0).astype(BF16)))
+                for g in range(NG):
+                    store(g, h, wp, jnp.concatenate([p[SUB * g:SUB * g + SUB] for p in px], axis=I0).astype(BF16))
+            return carry
+        lax.fori_loop(I0, TILEH, step, I0)
+
+    def put(dst, h, hb):
+        return pltpu.make_async_copy(io.at[:, hb * TILEH + h], dst.at[:, hb * TILEH + h], io_sem.at[h + TILEH * hb])
+
+    def unload_tiles(src, dst):
+        def step(h, carry):
+            for wp in range(QUAD):
+                v = [src[g, QUAD * h + wp].astype(F32) for g in range(NG)]
+                for q in range(PAIR):
+                    m = jnp.transpose(jnp.concatenate([p[SUB * q:SUB * q + SUB] for p in v], axis=I0))
+                    for j in range(SUB):
+                        at = (j // QUAD) * 1056 + (j % QUAD) * SUB + PAIR * wp + q
+                        xf[pl.ds(at, IMG, stride=33), :] = m[IMG * j:IMG * j + IMG]
+            for hb in range(PAIR):
+                for b in range(IMG):
+                    at = hb * 1056 + b * 33
+                    io[b, hb * TILEH + h] = xf[at:at + IMG, :].astype(BF16)
+                put(dst, h, hb).start()
+            return carry
+        lax.fori_loop(I0, TILEH, step, I0)
+
+    def unload_wait(dst):
+        for h in range(TILEH):
+            for hb in range(PAIR):
+                put(dst, h, hb).wait()
 
     def col(k, off, n, width):
         piece = cols[k, off:off + n, :]
@@ -350,6 +376,8 @@
             h = (dot(w1t[k], nb) + col(k, FC1B, HID, PXP)).astype(BF16)
             hbuf[k, i] = h
             g = gelu_of(h.astype(F32))
+            if k == I0:
+                g0buf[i] = g
             if with_cross:
                 cr = drbuf[i].astype(F32) * g
                 acc_cross[...] += cr[:, I0:PXL] + cr[:, PXL:PXP]
@@ -377,7 +405,7 @@
 
     def block1_out():
         def step(i, carry):
-            r = resp_of(I0, gelu_of(hbuf[I0, i].astype(F32)))
+            r = resp_of(I0, g0buf[i])
             hh, wp = i // QUAD, lax.rem(i, QUAD)
             res = [x1[g, RAD + hh, PAIR + wp].astype(F32).reshape(PAIR, SUB, PXL) for g in range(NG)]
             y = project(I0, i, r, res)
@@ -397,9 +425,17 @@
             drbuf[i] = dr
             dr = dr.astype(F32)
             if with_cross:
-                cr = dr * gelu_of(hbuf[k, i].astype(F32))
+                cr = dr * g0buf[i]
                 acc_cross[...] += cr[:, I0:PXL] + cr[:, PXL:PXP]
             acc_beta[...] += dr[:, I0:PXL] + dr[:, PXL:PXP]
+            return carry
+        lax.fori_loop(I0, NPAIR, step, I0, unroll=QUAD)
+
+    def slope_phase(k):
+        def step(i, carry):
+            x = hbuf[k, i].astype(F32)
+            phi = 0.5 + 0.5 * lax.erf(x * 0.7071067811865476)
+            slbuf[i] = phi + (x * 0.3989422804014327) * jnp.exp(-0.5 * (x * x))
             return carry
         lax.fori_loop(I0, NPAIR, step, I0, unroll=QUAD)
 
@@ -418,23 +454,20 @@
 
         def step(i, carry):
             hh, wp = i // QUAD, lax.rem(i, QUAD)
-            x = hbuf[k, i].astype(F32)
-            phi = 0.5 + 0.5 * lax.erf(x * 0.7071067811865476)
-            g = x * phi
-            slope = phi + (x * 0.3989422804014327) * jnp.exp(-0.5 * (x * x))
+            g = gelu_of(hbuf[k, i].astype(F32)) if k == I1 else g0buf[i]
             r = resp_of(k, g)
             if with_out:
                 res = [x2[g_, RAD + hh, PAIR + wp].astype(F32).reshape(PAIR, SUB, PXL) for g_ in range(NG)]
                 y = project(k, i, r, res)
                 for g_ in range(NG):
-                    y_out[g_, i] = y[g_]
+                    ytile[g_, i] = y[g_]
             dm = to_mat(load_pair(dy, i))
             dz = jnp.where(mask_row(k) > ZERO, dm, ZERO)
             dz = jnp.concatenate([dz, jnp.zeros((SUB, PXP), F32)], axis=I0).astype(BF16)
             nb = nbuf[k, i]
             rhs = jnp.concatenate([nb, dz], axis=I0)
             dga = drbuf[i].astype(F32) * wide(sbuf[k], PXP) + g * wide(qbuf[...], PXP)
-            dh = (dga * slope).astype(BF16)
+            dh = (dga * slbuf[i]).astype(BF16)
             raug = jnp.concatenate([r, jnp.ones((PR, PXP), BF16)], axis=I0)
             acc_f1[...] += nt_dot(dh, rhs)
             acc_f2[...] += nt_dot(raug, rhs)
@@ -504,12 +537,19 @@
             out[g, pl.ds(SUB * hp, SUB)] = v.astype(BF16)
         conv(dp, finish)
 
-    def to_x1(g, i, v):
-        x1[g, RAD + i // QUAD, PAIR + lax.rem(i, QUAD)] = v
-
-    def to_gout(g, i, v):
-        gout[g, i] = v
-    load_tiles(xin, to_x1)
+    def to_x1(g, h, wp, v):
+        x1[g, RAD + h, PAIR + wp] = v
+
+    def to_gout(g, h, wp, v):
+        gout[g, QUAD * h + wp] = v
+    for c in range(QUAD):
+        fetch(xin, c).start()
+    for c in range(QUAD):
+        fetch(xin, c).wait()
+    load_tiles(to_x1)
+    for c in range(QUAD):
+        fetch(gin, c).start()
+    pl.semaphore_wait(barrier, TAP)
     halo_start(x1, I0)
     setup()
     build_band(I0, I0)
@@ -518,7 +558,9 @@
     hidden_forward(I0, False)
     sa[I0, I0:CH] = pack_sums(fold(acc_g2))
     reduce_start(I0, CH)
-    load_tiles(gin, to_gout)
+    for c in range(QUAD):
+        fetch(gin, c).wait()
+    load_tiles(to_gout)
     build_band(I0, I1)
     total = reduce_finish(I0, CH)
     scale_from(I0, total)
@@ -532,6 +574,7 @@
     sa[I1, CH:80] = pack_sums(fold(acc_cross))
     reduce_start(I1, 80)
     build_band(I1, I1)
+    slope_phase(I1)
     total = reduce_finish(I1, 80)
     scale_from(I1, total[I0:CH])
     grn_grad(I1, total[CH:80])
@@ -539,12 +582,14 @@
     halo_start(dp, PAIR)
     conv_wgrad(I1, x2)
     store_grads(I1)
+    unload_tiles(ytile, act_out)
     halo_finish(dp, PAIR)
     conv_backward(gout, dmid)
     resp_phase(I0, dmid, True)
     sa[PAIR, I0:CH] = pack_sums(fold(acc_cross))
     reduce_start(PAIR, CH)
     build_band(I1, I0)
+    slope_phase(I0)
     total = reduce_finish(PAIR, CH)
     grn_grad(I0, total)
     hidden_backward(I0, dmid, False)
@@ -561,7 +606,7 @@
     for c in scat:
         c.start()
     halo_finish(dp, RAD)
-    conv_backward(dmid, dx_out)
+    conv_backward(dmid, dmid)
     for c in scat:
         c.wait()
     mine = gb[me // QUAD, pl.ds(pl.multiple_of(lax.rem(me, QUAD) * 56, SUB), 56), :]
@@ -573,31 +618,60 @@
         device_id=peer(d), device_id_type=MESH) for d in range(I1, SUB)]
     for c in gath:
         c.start()
+    unload_wait(act_out)
+    unload_tiles(dmid, grad_in)
     for c in gath:
         c.wait()
-    gr_out[me] = gs[TAP]
+    grf[me] = gs[TAP]
     for d in range(I1, SUB):
-        gr_out[lax.rem(me + SUB - d, SUB)] = gs[d - I1]
+        grf[lax.rem(me + SUB - d, SUB)] = gs[d - I1]
+    for k in range(PAIR):
+        gb[k] = grf[QUAD * k:QUAD * k + QUAD].reshape(ROWS, LANE)
+    for k in range(PAIR):
+        t = jnp.transpose(gb[k, I0:HID, :])
+        o_w1[k] = t[I0:CH]
+        o_w2[k] = t[CHP:CHQ] * KEEP
+        o_b1[k:k + I1, :] = t[CH:41]
+        o_beta[k:k + I1, :] = t[CHQ:89]
+        o_gamma[k:k + I1, :] = t[89:90]
+        o_gnorm[k:k + I1, :] = t[90:91, I0:CH]
+        o_bnorm[k:k + I1, :] = t[91:92, I0:CH]
+        o_bconv[k:k + I1, :] = t[92:93, I0:CH]
+        o_b2[k:k + I1, :] = gb[k, HID:161, CHP:CHQ] * KEEP
+    place = lax.broadcasted_iota(jnp.int32, (PAIR, LANE), I1) // SUB
+
+    def taps_row(i, carry):
+        for j in range(TAP):
+            out = jnp.zeros((PAIR, LANE), F32)
+            for g in range(NG):
+                rows = jnp.concatenate([gb[k, pl.ds(HIDP + SUB * g + i, I1), :] for k in range(PAIR)], axis=I0)
+                out = jnp.where(place == g, pltpu.roll(rows, (LANE + SUB * (g - j)) % LANE, I1), out)
+            o_taps[i, j] = out[:, I0:CH]
+        return carry
+    lax.fori_loop(I0, TAP, taps_row, I0)
+    unload_wait(grad_in)
 
 
 def run_kernel(args):
-    act = jax.ShapeDtypeStruct((NG, NPAIR, PR, PXL), BF16)
     vm = pl.BlockSpec(memory_space=pltpu.VMEM)
+    hbm = pl.BlockSpec(memory_space=pl.ANY)
     pad = pltpu.VMEM((NG, PADH, SUB, PR, PXL), BF16)
+    tiles = pltpu.VMEM((NG, NPAIR, PR, PXL), BF16)
     return pl.pallas_call(
         kernel,
         name='blocks',
-        out_shape=(act, act, jax.ShapeDtypeStruct((SUB, 56, LANE), F32)),
-        in_specs=[vm] * len(args),
-        out_specs=(vm, vm, vm),
+        out_shape=out_shapes(),
+        in_specs=[hbm] * PAIR + [vm] * (len(args) - PAIR),
+        out_specs=(hbm,) * PAIR + (vm,) * 10,
         scratch_shapes=[
-            pltpu.VMEM((IMG * 385, CH), F32), pltpu.VMEM((NG, NPAIR, PR, PXL), BF16),
+            pltpu.VMEM((IMG, PADH, IMG, CH), BF16), pltpu.VMEM((2112, CH), F32), tiles, tiles,
             pltpu.VMEM((PAIR, SUB, PXL), F32), pltpu.VMEM((PAIR, NG, SUB, SUB, LANE), F32), pltpu.VMEM((PAIR, 640, LANE), F32),
             pltpu.VMEM((PAIR, HID, CHP), BF16), pltpu.VMEM((PAIR, HID, CH), BF16),
             pad, pad, pad,
             pltpu.VMEM((PAIR, NG, NPAIR, PR, PXL), BF16),
             pltpu.VMEM((PAIR, NPAIR, CHP, PXP), BF16),
             pltpu.VMEM((PAIR, NPAIR, HID, PXP), BF16),
+            pltpu.VMEM((NPAIR, HID, PXP), F32), pltpu.VMEM((NPAIR, HID, PXP), F32),
             pltpu.VMEM((NPAIR, HID, PXP), BF16),
             pltpu.VMEM((NG, NPAIR, PR, PXL), BF16),
             pltpu.VMEM((NG, LANE, BAND), BF16),
@@ -609,73 +683,53 @@
             pltpu.VMEM((QUAD, NG, RAD, QUAD, PR, LANE), BF16), pltpu.VMEM((QUAD, NG, RAD, QUAD, PR, LANE), BF16),
             pltpu.VMEM((QUAD, 18, CH, LANE), BF16), pltpu.VMEM((QUAD, PADH, CH, LANE), BF16),
             pltpu.VMEM((RAD, 80, LANE), F32), pltpu.VMEM((RAD, TAP, 80, LANE), F32),
-            pltpu.VMEM((PAIR, ROWS, LANE), F32), pltpu.VMEM((TAP, 56, LANE), F32), pltpu.VMEM((SUB, 56, LANE), F32),
+            pltpu.VMEM((PAIR, ROWS, LANE), F32), pltpu.VMEM((TAP, 56, LANE), F32), pltpu.VMEM((SUB, 56, LANE), F32), pltpu.VMEM((SUB, 56, LANE), F32),
+            pltpu.SemaphoreType.DMA((PADH,)),
             pltpu.SemaphoreType.DMA((QUAD, NG)), pltpu.SemaphoreType.DMA((QUAD, NG)),
             pltpu.SemaphoreType.DMA((RAD, TAP)), pltpu.SemaphoreType.DMA((RAD, TAP)),
             pltpu.SemaphoreType.DMA((TAP,)), pltpu.SemaphoreType.DMA((TAP,)),
             pltpu.SemaphoreType.DMA((TAP,)), pltpu.SemaphoreType.DMA((TAP,)),
         ],
-        compiler_params=pltpu.CompilerParams(collective_id=I0, has_side_effects=True, vmem_limit_bytes=60 * PAIR**20),
+        compiler_params=pltpu.CompilerParams(collective_id=I0, has_side_effects=True, vmem_limit_bytes=67043328),
     )(*args)
 
 
-def finish_kernel(y, dx, gr, act_out, grad_in, o_taps, o_bconv, o_gnorm, o_bnorm, o_w1, o_b1, o_gamma, o_beta, o_w2, o_b2, yf):
-    def unload(src, dst, n):
-        for wp in range(QUAD):
-            v = [src[g, wp].astype(F32) for g in range(NG)]
-            for q in range(PAIR):
-                m = jnp.transpose(jnp.concatenate([p[SUB * q:SUB * q + SUB] for p in v], axis=I0))
-                for j in range(SUB):
-                    at = (j // QUAD) * 1056 + (j % QUAD) * SUB + PAIR * wp + q
-                    yf[n, pl.ds(at, IMG, stride=33), :] = m[IMG * j:IMG * j + IMG]
-        for hb in range(PAIR):
-            for b in range(IMG):
-                at = hb * 1056 + b * 33
-                dst[b, hb, I0] = yf[n, at:at + IMG, :].astype(BF16)
-    unload(y, act_out, I0)
-    unload(dx, grad_in, I1)
-
-    @pl.when(pl.program_id(I0) == I0)
-    def _():
-        for k in range(PAIR):
-            t = jnp.transpose(gr[k, I0:HID, :])
-            o_w1[k] = t[I0:CH]
-            o_w2[k] = t[CHP:CHQ] * KEEP
-            o_b1[k:k + I1, :] = t[CH:41]
-            o_beta[k:k + I1, :] = t[CHQ:89]
-            o_gamma[k:k + I1, :] = t[89:90]
-            o_gnorm[k:k + I1, :] = t[90:91, I0:CH]
-            o_bnorm[k:k + I1, :] = t[91:92, I0:CH]
-            o_bconv[k:k + I1, :] = t[92:93, I0:CH]
-            o_b2[k:k + I1, :] = gr[k, HID:161, CHP:CHQ] * KEEP
-        place = lax.broadcasted_iota(jnp.int32, (PAIR, LANE), I1) // SUB
-
-        def taps_row(i, carry):
-            for j in range(TAP):
-                out = jnp.zeros((PAIR, LANE), F32)
-                for g in range(NG):
-                    rows = jnp.concatenate([gr[k, pl.ds(HIDP + SUB * g + i, I1), :] for k in range(PAIR)], axis=I0)
-                    out = jnp.where(place == g, pltpu.roll(rows, (LANE + SUB * (g - j)) % LANE, I1), out)
-                o_taps[i, j] = out[:, I0:CH]
-            return carry
-        lax.fori_loop(I0, TAP, taps_row, I0)
-
-
-def finish(y, dx, gr):
+def out_shapes():
     shape = lambda *d: jax.ShapeDtypeStruct(d, F32)
-    act = jax.ShapeDtypeStruct((IMG, PAIR, TILEH, IMG, CH), BF16)
+    act = jax.ShapeDtypeStruct((IMG, PADH, IMG, CH), BF16)
     small, wide = shape(PAIR, CH), shape(PAIR, HID)
-    tile = pl.BlockSpec((NG, QUAD, PR, PXL), lambda h: (I0, h, I0, I0))
-    rows = pl.BlockSpec((IMG, PAIR, I1, IMG, CH), lambda h: (I0, I0, h, I0, I0))
-    whole = lambda o: pl.BlockSpec(o.shape, lambda h: (I0,) * len(o.shape))
-    grads = (shape(TAP, TAP, PAIR, CH), small, small, small, shape(PAIR, CH, HID), wide, wide, wide, shape(PAIR, CH, HID), small)
+    return (act, act, shape(TAP, TAP, PAIR, CH), small, small, small, shape(PAIR, CH, HID), wide, wide, wide, shape(PAIR, CH, HID), small)
+
+
+def finish_kernel(*refs):
+    n = len(refs) // RAD
+    src, dst, mid = refs[I0:n], refs[n:PAIR * n], refs[PAIR * n:RAD * n]
+    in_sem, out_sem = refs[RAD * n:]
+    moves = []
+    for a in range(n):
+        cuts = [slice(SUB * c, SUB * c + SUB) for c in range(QUAD)] if a < PAIR else [slice(None)]
+        for cut in cuts:
+            moves.append((src[a].at[cut], mid[a].at[cut], dst[a].at[cut]))
+    ins = [pltpu.make_async_copy(m[I0], m[I1], in_sem.at[c]) for c, m in enumerate(moves)]
+    outs = [pltpu.make_async_copy(m[I1], m[PAIR], out_sem.at[c]) for c, m in enumerate(moves)]
+    for c in ins:
+        c.start()
+    for c, o in zip(ins, outs):
+        c.wait()
+        o.start()
+    for o in outs:
+        o.wait()
+
+
+def finish(parts):
+    n = len(parts)
+    hbm = pl.BlockSpec(memory_space=pl.ANY)
     return pl.pallas_call(
-        finish_kernel, name='finish', grid=(TILEH,),
-        out_shape=(act, act) + grads,
-        in_specs=[tile, tile, whole(gr)], out_specs=(rows, rows) + tuple(whole(o) for o in grads),
-        scratch_shapes=[pltpu.VMEM((PAIR, 2112, CH), F32)],
-        compiler_params=pltpu.CompilerParams(vmem_limit_bytes=60 * PAIR**20),
-    )(y, dx, gr)
+        finish_kernel, name='finish', out_shape=out_shapes(),
+        in_specs=[hbm] * n, out_specs=(hbm,) * n,
+        scratch_shapes=[pltpu.VMEM(o.shape, o.dtype) for o in out_shapes()] + [pltpu.SemaphoreType.DMA((n + TILEH,))] * PAIR,
+        compiler_params=pltpu.CompilerParams(vmem_limit_bytes=67043328),
+    )(*parts)
 
 
 def solution(mesh):
@@ -683,11 +737,11 @@
     rep = P()
 
     def local_step(act_in, drop_mask, grad_out, conv_w, conv_b, norm_g, norm_b, fc1_w, fc1_b, grn_gamma, grn_beta, fc2_w, fc2_b):
-        y, dx, gr = run_kernel((act_in, grad_out, drop_mask.T, conv_w.transpose(I1, PAIR, I0, RAD), fc1_b, grn_gamma, grn_beta,
-                                conv_b, norm_g, norm_b, fc2_b, fc1_w, fc2_w.transpose(I0, PAIR, I1)))
-        act_out, grad_in, taps, *rest = finish(y, dx, gr.reshape(PAIR, ROWS, LANE))
+        parts = run_kernel((act_in, grad_out, drop_mask.T, conv_w.transpose(I1, PAIR, I0, RAD), fc1_b, grn_gamma, grn_beta,
+                            conv_b, norm_g, norm_b, fc2_b, fc1_w, fc2_w.transpose(I0, PAIR, I1)))
+        act_out, grad_in, taps, *rest = finish(parts)
         rest[TAP] = rest[TAP].transpose(I0, PAIR, I1)
-        return (act_out.reshape(IMG, PADH, IMG, CH), grad_in.reshape(IMG, PADH, IMG, CH), taps.transpose(PAIR, I0, I1, RAD), *rest)
+        return (act_out, grad_in, taps.transpose(PAIR, I0, I1, RAD), *rest)
 
     return jax.shard_map(local_step, mesh=mesh,
                          in_specs=(act_spec, P('dp', None), act_spec) + (rep,) * 10,

time: 106 us -> 94.5 us (0.89)
  Pallas kernels: 105 us -> 93.5 us
    pallas_call x2, Pallas kernels: 105 us -> 93.5 us  [the longest x1 87.7 us: run_kernel(): pl.pallas_call(kernel, name='blocks', out_shape=out_shapes(), in_specs=[h...]
where the time goes in v3:
time: 94.5 us; the launch traced here: 94.3 us
  Pallas kernels  93.5 us (99%)
    pallas_call x1, Pallas kernels, run_kernel(): pl.pallas_call(kernel, name='blocks', out_shape=out_shapes(), in_specs=[h...  87.7 us
    pallas_call x1, Pallas kernels, finish(): pl.pallas_call(finish_kernel, name='finish', out_shape=out_shapes(), in_s...  5.76 us

profile of v3, /device:TPU:0, one launch (start us, length us, event | category | flops | bytes accessed | tf_op | source)
XLA Modules:
  0.0 94.3 jit_solution(13850776967136707236)
XLA Ops:
  0.6 87.7 %blocks.1 = (bf16[32,12,32,40]{3,2,1,0:T(8,128)(2,1)}, bf16[32,12,32,40]{3,2,1,0:T(8,128)(2,1)}, f32[7,7,2,40]{3,2,1,0:T(2,128)}, f32[2,40]{1,0:T(2,128)}, f32[2...) custom-call(bf16[32,12,32,40]{3,2,1,0:T(8,128)(2,1)} %xin.1, ...), custom_call_target="tpu_custom_call" | custom-call | tf_op jit(solution)/shard_map/blocks/pallas_call | solution.py:660
  88.4 5.8 %finish.1 = (bf16[32,12,32,40]{3,2,1,0:T(8,128)(2,1)}, bf16[32,12,32,40]{3,2,1,0:T(8,128)(2,1)}, f32[7,7,2,40]{3,2,1,0:T(2,128)}, f32[2,40]{1,0:T(2,128)}, f32[2...) custom-call(bf16[32,12,32,40]{3,2,1,0:T(8,128)(2,1)} %get-tuple-elem, ...), custom_call_target="tpu_custom_call" | custom-call | tf_op jit(solution)/shard_map/finish/pallas_call | solution.py:727

commit v4 on v3

--- a/solution.py
+++ b/solution.py
@@ -57,8 +57,8 @@
            act_out, grad_in, o_taps, o_bconv, o_gnorm, o_bnorm, o_w1, o_b1, o_gamma, o_beta, o_w2, o_b2,
            io, xf, gout, ytile, mask, eb, cols, w1t, w2, x1, x2, dp, dbuf, nbuf, hbuf, g0buf, slbuf, drbuf, dmid, tbuf,
            acc_g2, acc_cross, acc_beta, acc_n, acc_f1, acc_f2, gvec, sbuf, gnbuf, qbuf,
-           ru, rd, rc, sc, sa, ra, gb, grx, gs, grf,
-           io_sem, hs_sem, hr_sem, as_sem, ar_sem, gs_sem, gr_sem, as2_sem, ar2_sem):
+           ru, rd, rc, sc, sa, ra, gb, grx, gs, grf, tx, tsum,
+           io_sem, hs_sem, hr_sem, as_sem, ar_sem, gs_sem, gr_sem, as2_sem, ar2_sem, ts_sem, tr_sem):
     sw = lax.axis_index('sw')
     sh = lax.axis_index('sh')
     me = sw * QUAD + sh
@@ -168,9 +168,9 @@
         return (
             lambda: cp(src.at[:, TILEH:9, PAIR:TILEH, :, LANE:PXL], ru.at[e], I0, down),
             lambda: cp(src.at[:, RAD:TILEH, PAIR:TILEH, :, I0:LANE], rd.at[e], I1, up),
-            lambda: cp(sc.at[e], rc.at[e, RAD:15], PAIR, {'sw': other_w, 'sh': sh}),
-            lambda: cp(sc.at[e, 9:PADH], rc.at[e, I0:RAD], RAD, downx),
-            lambda: cp(sc.at[e, I0:RAD], rc.at[e, 15:18], QUAD, upx),
+            lambda: cp(sc.at[e], rc.at[e, I1:QUAD], PAIR, {'sw': other_w, 'sh': sh}),
+            lambda: cp(sc.at[e, PAIR:RAD], rc.at[e, I0:I1], RAD, downx),
+            lambda: cp(sc.at[e, I0:I1], rc.at[e, QUAD:NG], QUAD, upx),
         )
 
     def halo_start(src, e):
@@ -185,20 +185,22 @@
             copies[I1]().start()
         first = QUAD - PAIR * sw
 
-        def pack(h, carry):
-            for half in range(PAIR):
-                ls = slice(half * LANE, half * LANE + LANE)
-                pieces = []
-                for g in range(NG):
-                    v = src[g, RAD + h, pl.ds(first, PAIR), :, ls].astype(F32).reshape(QUAD, SUB, LANE)
-                    out = jnp.zeros((SUB, LANE), F32)
-                    for q in range(QUAD):
-                        shift = lax.rem(q * IMG + IMG * (I1 - sw), LANE)
-                        out = jnp.where(grp == q, pltpu.roll(v[q], shift, I1), out)
-                    pieces.append(out)
-                sc[e, TILEH * half + h] = jnp.concatenate(pieces, axis=I0).astype(BF16)
-            return carry
-        lax.fori_loop(I0, TILEH, pack, I0, unroll=PAIR)
+        on_left = jnp.where(sw == I0, ONE, ZERO)
+        on_right = jnp.where(sw == I1, ONE, ZERO)
+        turn = IMG * (I1 - sw)
+        for n in range(RAD):
+            unit = []
+            for a in range(QUAD * n, QUAD * n + QUAD):
+                ls = slice((a // TILEH) * LANE, (a // TILEH) * LANE + LANE)
+                v = src[:, RAD + a % TILEH, pl.ds(first, PAIR), :, ls].astype(F32).reshape(NG, QUAD, SUB, LANE)
+                unit += [v[:, c + I1] * on_left + v[:, c] * on_right for c in range(RAD)]
+            pieces = []
+            for p in range(RAD):
+                out = jnp.zeros((NG, SUB, LANE), F32)
+                for q in range(QUAD):
+                    out = jnp.where(grp[None] == q, pltpu.roll(unit[QUAD * p + q], lax.rem(q * IMG + turn, LANE), PAIR), out)
+                pieces.append(out.reshape(CH, LANE))
+            sc[e, n] = jnp.concatenate(pieces, axis=I0).astype(BF16)
         copies[PAIR]().start()
 
         @pl.when(sh < RAD)
@@ -212,12 +214,12 @@
         @pl.when(sh == I0)
         def _():
             ru[e] = jnp.zeros(ru.shape[I1:], BF16)
-            rc[e, I0:RAD] = jnp.zeros((RAD, CH, LANE), BF16)
+            rc[e, I0] = jnp.zeros((120, LANE), BF16)
 
         @pl.when(sh == RAD)
         def _():
             rd[e] = jnp.zeros(rd.shape[I1:], BF16)
-            rc[e, 15:18] = jnp.zeros((RAD, CH, LANE), BF16)
+            rc[e, QUAD] = jnp.zeros((120, LANE), BF16)
 
     def halo_finish(src, e):
         copies = halo_copies(src, e)
@@ -237,32 +239,55 @@
             copies[RAD]().wait_recv()
         copies[PAIR]().wait()
         for r in range(RAD):
+            src[:, r, PAIR:TILEH, :, I0:LANE] = ru[e, :, r]
+            src[:, 9 + r, PAIR:TILEH, :, LANE:PXL] = rd[e, :, r]
+        for r in range(RAD):
+            pad_row(src, r, I0)
+            pad_row(src, 9 + r, I1)
+        spot = lane128 - TQ * (I1 - sw)
+        edge_lanes = jnp.logical_and(spot >= I0, spot < IMG)[None]
+        side = TILEH - TILEH * sw
+        on_left = jnp.where(sw == I0, ONE, ZERO)
+        on_right = jnp.where(sw == I1, ONE, ZERO)
+        for quad in range(NG):
+            strip = rc[e, quad].astype(F32).reshape(RAD, NG, SUB, LANE)
+            for rr in range(QUAD):
+                spots = [(QUAD * quad + rr - I1 - TILEH * half, half) for half in range(PAIR)]
+                spots = [(h, half) for h, half in spots if I0 <= h < PADH]
+                edge = []
+                for q in range(QUAD if spots else I0):
+                    ua, ub = RAD * rr + max(q - I1, I0), RAD * rr + min(q, PAIR)
+                    shift = lax.rem(LANE - IMG * (ua % QUAD) + (I1 - sw) * (TQ + IMG * (ua % QUAD - ub % QUAD)), LANE)
+                    unit = strip[ua // QUAD]
+                    if ua // QUAD != ub // QUAD:
+                        unit = unit * on_right + strip[ub // QUAD] * on_left
+                    edge.append(pltpu.roll(unit, shift, PAIR))
+                for h, half in spots:
+                    ls = slice(half * LANE, half * LANE + LANE)
+                    old = src[:, h, pl.ds(side, PAIR), :, ls].astype(F32).reshape(NG, QUAD, SUB, LANE)
+                    new = [jnp.where(edge_lanes, edge[q], old[:, q])[:, None] for q in range(QUAD)]
+                    src[:, h, pl.ds(side, PAIR), :, ls] = jnp.concatenate(new, axis=I1).reshape(NG, PAIR, PR, LANE).astype(BF16)
+
+    def pad_row(src, h, half):
+        ls = slice(half * LANE, half * LANE + LANE)
+        lanes = lane128[None, None]
+        hi = src[:, h, QUAD:TILEH, :, ls].astype(F32).reshape(NG, QUAD, SUB, LANE)
+        lo = src[:, h, PAIR:QUAD, :, ls].astype(F32).reshape(NG, QUAD, SUB, LANE)
+        left = jnp.where(lanes < IMG, ZERO, pltpu.roll(hi, IMG, RAD))
+        right = jnp.where(lanes >= TQ, ZERO, pltpu.roll(lo, TQ, RAD))
+        src[:, h, I0:PAIR, :, ls] = left.reshape(NG, PAIR, PR, LANE).astype(BF16)
+        src[:, h, TILEH:SUB, :, ls] = right.reshape(NG, PAIR, PR, LANE).astype(BF16)
+
+    def halo_local(src):
+        for r in range(RAD):
             src[:, r, PAIR:TILEH, :, LANE:PXL] = src[:, TILEH + r, PAIR:TILEH, :, I0:LANE]
-            src[:, r, PAIR:TILEH, :, I0:LANE] = ru[e, :, r]
             src[:, 9 + r, PAIR:TILEH, :, I0:LANE] = src[:, RAD + r, PAIR:TILEH, :, LANE:PXL]
-            src[:, 9 + r, PAIR:TILEH, :, LANE:PXL] = rd[e, :, r]
-        is_left = (lane128 < IMG)
-        is_right = (lane128 >= TQ)
-        keep_left = jnp.where(sw == I1, ONE, ZERO)
-        keep_right = jnp.where(sw == I0, ONE, ZERO)
-
-        def pad(h, carry):
-            for half in range(PAIR):
-                ls = slice(half * LANE, half * LANE + LANE)
-                strip = rc[e, h + TILEH * half].astype(F32).reshape(NG, SUB, LANE)
-                for g in range(NG):
-                    hi = src[g, h, QUAD:TILEH, :, ls].astype(F32).reshape(QUAD, SUB, LANE)
-                    lo = src[g, h, PAIR:QUAD, :, ls].astype(F32).reshape(QUAD, SUB, LANE)
-                    left, right = [], []
-                    for q in range(QUAD):
-                        shift = lax.rem(jnp.where(sw == I1, LANE - q * IMG, 224 - q * IMG), LANE)
-                        edge = pltpu.roll(strip[g], shift, I1)
-                        left.append(jnp.where(is_left, edge * keep_left, pltpu.roll(hi[q], IMG, I1)))
-                        right.append(jnp.where(is_right, edge * keep_right, pltpu.roll(lo[q], TQ, I1)))
-                    src[g, h, I0:PAIR, :, ls] = jnp.concatenate(left, axis=I0).reshape(PAIR, PR, LANE).astype(BF16)
-                    src[g, h, TILEH:SUB, :, ls] = jnp.concatenate(right, axis=I0).reshape(PAIR, PR, LANE).astype(BF16)
-            return carry
-        lax.fori_loop(I0, PADH, pad, I0, unroll=PAIR)
+
+        def pad(u, carry):
+            pad_row(src, RAD + u, I0)
+            pad_row(src, u, I1)
+            return carry
+        lax.fori_loop(I0, 9, pad, I0, unroll=RAD)
 
     def fold(ref):
         v = ref[:, I0:LANE] + ref[:, LANE:PXL]
@@ -507,7 +532,7 @@
                     out = out + pltpu.roll(gvec[at:at + SUB, :], BAND - (h * LANE + (w + I1) * SUB), I1)
             out = jnp.sum(jnp.where(sub == lane, out, ZERO), axis=I0, keepdims=True)
             rows = jnp.concatenate([out[:, LANE * i:LANE * i + LANE] for i in range(SUB)], axis=I0)
-            gb[k, pl.ds(HIDP + SUB * g, SUB), :] = rows
+            tx[k, me, pl.ds(SUB * g, SUB), :] = rows
             return carry
         lax.fori_loop(I0, NG, one, I0, unroll=NG)
 
@@ -529,13 +554,45 @@
         for j in range(RAD):
             out = out + column(acc_n[j, :, I0:LANE] + acc_n[j, :, LANE:PXL], 90 + j, CH)
         gb[k, I0:HIDP, :] = out
-        gb[k, 216:224, :] = jnp.zeros((SUB, LANE), F32)
+        gb[k, HIDP:192, :] = jnp.zeros((PR, LANE), F32)
 
     def conv_backward(dy, out):
         def finish(g, hp, acc):
             v = acc.reshape(SUB, PR, PXL) + dy[g, pl.ds(SUB * hp, SUB)].astype(F32)
             out[g, pl.ds(SUB * hp, SUB)] = v.astype(BF16)
         conv(dp, finish)
+
+    def scatter_copies(k):
+        return [pltpu.make_async_remote_copy(
+            src_ref=gb.at[k, pl.ds(pl.multiple_of(lax.rem(me + d, SUB) * NPAIR, SUB), NPAIR)], dst_ref=grx.at[k, d - I1],
+            send_sem=gs_sem.at[k, d - I1], recv_sem=gr_sem.at[k, d - I1],
+            device_id=peer(d), device_id_type=MESH) for d in range(I1, SUB)]
+
+    def gather_copies(k):
+        return [pltpu.make_async_remote_copy(
+            src_ref=gs.at[k, TAP], dst_ref=gs.at[k, d - I1], send_sem=as2_sem.at[k, d - I1], recv_sem=ar2_sem.at[k, d - I1],
+            device_id=peer(d), device_id_type=MESH) for d in range(I1, SUB)]
+
+    def tap_copies(k):
+        return [pltpu.make_async_remote_copy(
+            src_ref=tx.at[k, me], dst_ref=tx.at[k, me], send_sem=ts_sem.at[k, d - I1], recv_sem=tr_sem.at[k, d - I1],
+            device_id=peer(d), device_id_type=MESH) for d in range(I1, SUB)]
+
+    def start_all(copies):
+        for c in copies:
+            c.start()
+
+    def wait_all(copies):
+        for c in copies:
+            c.wait()
+
+    def scatter_to_gather(k):
+        wait_all(scatter_copies(k))
+        mine = gb[k, pl.ds(pl.multiple_of(me * NPAIR, SUB), NPAIR), :]
+        for d in range(TAP):
+            mine = mine + grx[k, d]
+        gs[k, TAP] = mine
+        start_all(gather_copies(k))
 
     def to_x1(g, h, wp, v):
         x1[g, RAD + h, PAIR + wp] = v
@@ -553,6 +610,7 @@
     halo_start(x1, I0)
     setup()
     build_band(I0, I0)
+    halo_local(x1)
     halo_finish(x1, I0)
     conv_forward(I0, x1)
     hidden_forward(I0, False)
@@ -566,6 +624,7 @@
     scale_from(I0, total)
     block1_out()
     halo_start(x2, I1)
+    halo_local(x2)
     resp_phase(I1, gout, False)
     halo_finish(x2, I1)
     conv_forward(I1, x2)
@@ -580,53 +639,45 @@
     grn_grad(I1, total[CH:80])
     hidden_backward(I1, gout, True)
     halo_start(dp, PAIR)
+    halo_local(dp)
     conv_wgrad(I1, x2)
     store_grads(I1)
-    unload_tiles(ytile, act_out)
     halo_finish(dp, PAIR)
+    start_all(scatter_copies(I1))
+    start_all(tap_copies(I1))
     conv_backward(gout, dmid)
     resp_phase(I0, dmid, True)
     sa[PAIR, I0:CH] = pack_sums(fold(acc_cross))
     reduce_start(PAIR, CH)
     build_band(I1, I0)
     slope_phase(I0)
+    unload_tiles(ytile, act_out)
     total = reduce_finish(PAIR, CH)
     grn_grad(I0, total)
+    scatter_to_gather(I1)
     hidden_backward(I0, dmid, False)
     halo_start(dp, RAD)
+    store_grads(I0)
+    start_all(scatter_copies(I0))
     conv_wgrad(I0, x1)
-    store_grads(I0)
-
-    def part(f):
-        return gb.at[f // QUAD, pl.ds(pl.multiple_of(lax.rem(f, QUAD) * 56, SUB), 56)]
-
-    scat = [pltpu.make_async_remote_copy(
-        src_ref=part(lax.rem(me + d, SUB)), dst_ref=grx.at[d - I1], send_sem=gs_sem.at[d - I1], recv_sem=gr_sem.at[d - I1],
-        device_id=peer(d), device_id_type=MESH) for d in range(I1, SUB)]
-    for c in scat:
-        c.start()
+    start_all(tap_copies(I0))
+    halo_local(dp)
+    scatter_to_gather(I0)
     halo_finish(dp, RAD)
     conv_backward(dmid, dmid)
-    for c in scat:
-        c.wait()
-    mine = gb[me // QUAD, pl.ds(pl.multiple_of(lax.rem(me, QUAD) * 56, SUB), 56), :]
-    for d in range(TAP):
-        mine = mine + grx[d]
-    gs[TAP] = mine
-    gath = [pltpu.make_async_remote_copy(
-        src_ref=gs.at[TAP], dst_ref=gs.at[d - I1], send_sem=as2_sem.at[d - I1], recv_sem=ar2_sem.at[d - I1],
-        device_id=peer(d), device_id_type=MESH) for d in range(I1, SUB)]
-    for c in gath:
-        c.start()
     unload_wait(act_out)
     unload_tiles(dmid, grad_in)
-    for c in gath:
-        c.wait()
-    grf[me] = gs[TAP]
-    for d in range(I1, SUB):
-        grf[lax.rem(me + SUB - d, SUB)] = gs[d - I1]
     for k in range(PAIR):
-        gb[k] = grf[QUAD * k:QUAD * k + QUAD].reshape(ROWS, LANE)
+        wait_all(tap_copies(k))
+        wait_all(gather_copies(k))
+        total = tx[k, I0]
+        for d in range(I1, SUB):
+            total = total + tx[k, d]
+        tsum[k] = total
+        grf[k, me] = gs[k, TAP]
+        for d in range(I1, SUB):
+            grf[k, lax.rem(me + SUB - d, SUB)] = gs[k, d - I1]
+        gb[k] = grf[k].reshape(192, LANE)
     for k in range(PAIR):
         t = jnp.transpose(gb[k, I0:HID, :])
         o_w1[k] = t[I0:CH]
@@ -644,7 +695,7 @@
         for j in range(TAP):
             out = jnp.zeros((PAIR, LANE), F32)
             for g in range(NG):
-                rows = jnp.concatenate([gb[k, pl.ds(HIDP + SUB * g + i, I1), :] for k in range(PAIR)], axis=I0)
+                rows = jnp.concatenate([tsum[k, pl.ds(SUB * g + i, I1), :] for k in range(PAIR)], axis=I0)
                 out = jnp.where(place == g, pltpu.roll(rows, (LANE + SUB * (g - j)) % LANE, I1), out)
             o_taps[i, j] = out[:, I0:CH]
         return carry
@@ -681,15 +732,14 @@
             pltpu.VMEM((LANE, BAND), F32),
             pltpu.VMEM((PAIR, HID, LANE), F32), pltpu.VMEM((PAIR, HID, LANE), F32), pltpu.VMEM((HID, LANE), F32),
             pltpu.VMEM((QUAD, NG, RAD, QUAD, PR, LANE), BF16), pltpu.VMEM((QUAD, NG, RAD, QUAD, PR, LANE), BF16),
-            pltpu.VMEM((QUAD, 18, CH, LANE), BF16), pltpu.VMEM((QUAD, PADH, CH, LANE), BF16),
+            pltpu.VMEM((QUAD, NG, 120, LANE), BF16), pltpu.VMEM((QUAD, RAD, 120, LANE), BF16),
             pltpu.VMEM((RAD, 80, LANE), F32), pltpu.VMEM((RAD, TAP, 80, LANE), F32),
-            pltpu.VMEM((PAIR, ROWS, LANE), F32), pltpu.VMEM((TAP, 56, LANE), F32), pltpu.VMEM((SUB, 56, LANE), F32), pltpu.VMEM((SUB, 56, LANE), F32),
+            pltpu.VMEM((PAIR, 192, LANE), F32), pltpu.VMEM((PAIR, TAP, NPAIR, LANE), F32), pltpu.VMEM((PAIR, SUB, NPAIR, LANE), F32),
+            pltpu.VMEM((PAIR, SUB, NPAIR, LANE), F32), pltpu.VMEM((PAIR, SUB, CH, LANE), F32), pltpu.VMEM((PAIR, CH, LANE), F32),
             pltpu.SemaphoreType.DMA((PADH,)),
             pltpu.SemaphoreType.DMA((QUAD, NG)), pltpu.SemaphoreType.DMA((QUAD, NG)),
             pltpu.SemaphoreType.DMA((RAD, TAP)), pltpu.SemaphoreType.DMA((RAD, TAP)),
-            pltpu.SemaphoreType.DMA((TAP,)), pltpu.SemaphoreType.DMA((TAP,)),
-            pltpu.SemaphoreType.DMA((TAP,)), pltpu.SemaphoreType.DMA((TAP,)),
-        ],
+        ] + [pltpu.SemaphoreType.DMA((PAIR, TAP))] * TILEH,
         compiler_params=pltpu.CompilerParams(collective_id=I0, has_side_effects=True, vmem_limit_bytes=67043328),
     )(*args)
 

time: 94.5 us -> 91.3 us (0.966)
  Pallas kernels: 93.5 us -> 90.3 us
    pallas_call x1, Pallas kernels: 87.7 us -> 84.5 us  [run_kernel(): pl.pallas_call(kernel, name='blocks', out_shape=out_shapes(), in_specs=[h...]
where the time goes in v4:
time: 91.3 us; the launch traced here: 91.1 us
  Pallas kernels  90.3 us (99%)
    pallas_call x1, Pallas kernels, run_kernel(): pl.pallas_call(kernel, name='blocks', out_shape=out_shapes(), in_specs=[h...  84.5 us
    pallas_call x1, Pallas kernels, finish(): pl.pallas_call(finish_kernel, name='finish', out_shape=out_shapes(), in_s...  5.76 us

profile of v4, /device:TPU:0, one launch (start us, length us, event | category | flops | bytes accessed | tf_op | source)
XLA Modules:
  0.0 91.1 jit_solution(3514380628680412257)
XLA Ops:
  0.6 84.5 %blocks.1 = (bf16[32,12,32,40]{3,2,1,0:T(8,128)(2,1)}, bf16[32,12,32,40]{3,2,1,0:T(8,128)(2,1)}, f32[7,7,2,40]{3,2,1,0:T(2,128)}, f32[2,40]{1,0:T(2,128)}, f32[2...) custom-call(bf16[32,12,32,40]{3,2,1,0:T(8,128)(2,1)} %xin.1, ...), custom_call_target="tpu_custom_call" | custom-call | tf_op jit(solution)/shard_map/blocks/pallas_call | solution.py:711
  85.2 5.8 %finish.1 = (bf16[32,12,32,40]{3,2,1,0:T(8,128)(2,1)}, bf16[32,12,32,40]{3,2,1,0:T(8,128)(2,1)}, f32[7,7,2,40]{3,2,1,0:T(2,128)}, f32[2,40]{1,0:T(2,128)}, f32[2...) custom-call(bf16[32,12,32,40]{3,2,1,0:T(8,128)(2,1)} %get-tuple-elem, ...), custom_call_target="tpu_custom_call" | custom-call | tf_op jit(solution)/shard_map/finish/pallas_call | solution.py:777

commit v5 on v4

--- a/solution.py
+++ b/solution.py
@@ -141,7 +141,7 @@
                     io[b, hb * TILEH + h] = xf[at:at + IMG, :].astype(BF16)
                 put(dst, h, hb).start()
             return carry
-        lax.fori_loop(I0, TILEH, step, I0)
+        lax.fori_loop(I0, TILEH, step, I0, unroll=PAIR)
 
     def unload_wait(dst):
         for h in range(TILEH):
@@ -287,7 +287,7 @@
             pad_row(src, RAD + u, I0)
             pad_row(src, u, I1)
             return carry
-        lax.fori_loop(I0, 9, pad, I0, unroll=RAD)
+        lax.fori_loop(I0, 9, pad, I0, unroll=9)
 
     def fold(ref):
         v = ref[:, I0:LANE] + ref[:, LANE:PXL]
@@ -757,7 +757,7 @@
     in_sem, out_sem = refs[RAD * n:]
     moves = []
     for a in range(n):
-        cuts = [slice(SUB * c, SUB * c + SUB) for c in range(QUAD)] if a < PAIR else [slice(None)]
+        cuts = [slice(QUAD * c, QUAD * c + QUAD) for c in range(SUB)] if a < PAIR else [slice(None)]
         for cut in cuts:
             moves.append((src[a].at[cut], mid[a].at[cut], dst[a].at[cut]))
     ins = [pltpu.make_async_copy(m[I0], m[I1], in_sem.at[c]) for c, m in enumerate(moves)]
@@ -777,7 +777,7 @@
     return pl.pallas_call(
         finish_kernel, name='finish', out_shape=out_shapes(),
         in_specs=[hbm] * n, out_specs=(hbm,) * n,
-        scratch_shapes=[pltpu.VMEM(o.shape, o.dtype) for o in out_shapes()] + [pltpu.SemaphoreType.DMA((n + TILEH,))] * PAIR,
+        scratch_shapes=[pltpu.VMEM(o.shape, o.dtype) for o in out_shapes()] + [pltpu.SemaphoreType.DMA((n + 14,))] * PAIR,
         compiler_params=pltpu.CompilerParams(vmem_limit_bytes=67043328),
     )(*parts)
 

time: 91.3 us -> 90.9 us (level)
  no operation moved by 1% of the time
where the time goes in v5:
time: 90.9 us; the launch traced here: 90.7 us
  Pallas kernels  89.9 us (99%)
    pallas_call x1, Pallas kernels, run_kernel(): pl.pallas_call(kernel, name='blocks', out_shape=out_shapes(), in_specs=[h...  84.1 us
    pallas_call x1, Pallas kernels, finish(): pl.pallas_call(finish_kernel, name='finish', out_shape=out_shapes(), in_s...  5.74 us

profile of v5, /device:TPU:0, one launch (start us, length us, event | category | flops | bytes accessed | tf_op | source)
XLA Modules:
  0.0 90.7 jit_solution(2835627551406178086)
XLA Ops:
  0.6 84.1 %blocks.1 = (bf16[32,12,32,40]{3,2,1,0:T(8,128)(2,1)}, bf16[32,12,32,40]{3,2,1,0:T(8,128)(2,1)}, f32[7,7,2,40]{3,2,1,0:T(2,128)}, f32[2,40]{1,0:T(2,128)}, f32[2...) custom-call(bf16[32,12,32,40]{3,2,1,0:T(8,128)(2,1)} %xin.1, ...), custom_call_target="tpu_custom_call" | custom-call | tf_op jit(solution)/shard_map/blocks/pallas_call | solution.py:711
  84.8 5.7 %finish.1 = (bf16[32,12,32,40]{3,2,1,0:T(8,128)(2,1)}, bf16[32,12,32,40]{3,2,1,0:T(8,128)(2,1)}, f32[7,7,2,40]{3,2,1,0:T(2,128)}, f32[2,40]{1,0:T(2,128)}, f32[2...) custom-call(bf16[32,12,32,40]{3,2,1,0:T(8,128)(2,1)} %get-tuple-elem, ...), custom_call_target="tpu_custom_call" | custom-call | tf_op jit(solution)/shard_map/finish/pallas_call | solution.py:777
